TPU v7x, 32 devices: a whole 2x2x4 slice. The times are simulated.
32 devices in a mesh: dp: 2 (over core), ctx: 4 (over z), tensor: 4 (over y, x).
Axes of the slice: x: 2, y: 2, z: 4, core: 2. Of those that a mesh axis runs over, the one named last changes fastest.
Arguments:
- tokens: bfloat16 [2, 1024, 2048], P('dp', 'ctx'), may hold values from -30 to 30
- segments: int32 [2, 1024], P('dp'), may hold values from 0 to 3, never falling along the last dimension, each value on 1 to 512 neighbouring positions
- first_gain: bfloat16 [2048], replicated, may hold values from 0.5 to 1.5
- query_weight: bfloat16 [2048, 2048], P(None, 'tensor'), may hold values from -0.125 to 0.125
- key_matrix: bfloat16 [2048, 1024], P(None, 'tensor'), may hold values from -0.125 to 0.125
- value_matrix: bfloat16 [2048, 1024], P(None, 'tensor'), may hold values from -0.125 to 0.125
- query_norm_gain: bfloat16 [128], replicated, may hold values from 0.5 to 1.5
- key_gain: bfloat16 [128], replicated, may hold values from 0.5 to 1.5
- output_weight: bfloat16 [2048, 2048], P('tensor'), may hold values from -1.5 to 1.5
- second_gain: bfloat16 [2048], replicated, may hold values from 0.5 to 1.5
- gate_weight: bfloat16 [2048, 6144], P(None, 'tensor'), may hold values from -0.125 to 0.125
- up_weight: bfloat16 [2048, 6144], P(None, 'tensor'), may hold values from -0.125 to 0.125
- down_weight: bfloat16 [6144, 2048], P('tensor'), may hold values from -0.078125 to 0.078125
- cotangent: bfloat16 [2, 1024, 2048], P('dp', 'ctx'), may hold values from -6 to 6
Outputs:
- outputs: bfloat16 [2, 1024, 2048], P('dp', 'ctx')
- token_grad: bfloat16 [2, 1024, 2048], P('dp', 'ctx')
- first_gain_grad: float32 [2048], replicated
- query_weight_grad: float32 [2048, 2048], P(('dp', 'ctx'), 'tensor')
- key_weight_grad: float32 [2048, 1024], P(('dp', 'ctx'), 'tensor')
- value_weight_grad: float32 [2048, 1024], P(('dp', 'ctx'), 'tensor')
- query_gain_grad: float32 [128], replicated
- key_gain_grad: float32 [128], replicated
- output_weight_grad: float32 [2048, 2048], P('tensor', ('dp', 'ctx'))
- second_gain_grad: float32 [2048], replicated
- gate_weight_grad: float32 [2048, 6144], P(('dp', 'ctx'), 'tensor')
- up_weight_grad: float32 [2048, 6144], P(('dp', 'ctx'), 'tensor')
- down_weight_grad: float32 [6144, 2048], P('tensor', ('dp', 'ctx'))
Inputs may be any that keep to these rules, and one draw needn't show every extreme that they name: `segments`: in each sequence the segment numbers never fall and every number of 0 to 3 appears; every document has 1 to 512 tokens and one has exactly 512.
All inputs are finite; a program needn't handle non-finite values.
Results may differ from a plain program's by a relative error of at most 0.03.
Values may be sent and summed in bfloat16 or wider, within the bound.
A program may use at most 192 MiB of HBM per device.

v0:
```python
import functools
import math

import jax
import jax.numpy as jnp
from jax import lax
from jax.experimental import pallas as pl
from jax.experimental.pallas import tpu as pltpu
from jax.sharding import PartitionSpec as P

epsilon = 1e-06
rope_base = 1000000.0
F32 = jnp.float32
BF16 = jnp.bfloat16
MESH = pl.DeviceIdType.MESH
TILE = 256


def dot(a, b):
    return jnp.dot(a, b, preferred_element_type=F32)


def dot_nt(a, b):
    return lax.dot_general(a, b, (((1,), (1,)), ((), ())), preferred_element_type=F32)


def dot_tn(a, b):
    return lax.dot_general(a, b, (((0,), (0,)), ((), ())), preferred_element_type=F32)


def remote(src, dst, send_sem, recv_sem, **device):
    return pltpu.make_async_remote_copy(
        src_ref=src,
        dst_ref=dst,
        send_sem=send_sem,
        recv_sem=recv_sem,
        device_id=device,
        device_id_type=MESH,
    )


def tiles(total, size, body):
    size = min(size, total)

    def step(i, _):
        body(pl.multiple_of(i * size, size), size)
        return 0

    lax.fori_loop(0, total // size, step, 0)


class Dims:
    pass


def layer_kernel(
    dm,
    tok_hbm,
    cot_hbm,
    g1,
    g2,
    gq,
    gk,
    cos,
    sin,
    qseg,
    kseg,
    qw_hbm,
    kw_hbm,
    vw_hbm,
    ow_hbm,
    gw_hbm,
    uw_hbm,
    dw_hbm,
    out_hbm,
    tgrad_hbm,
    gate_out,
    up_out,
    outw_out,
    hid_all,
    qkv_all,
    x1t_all,
    cott_all,
    gains_out,
    s,
):
    T, D, H, QH, KH, F, n, nt, reach, S, R = (
        dm.T, dm.D, dm.H, dm.QH, dm.KH, dm.F, dm.n, dm.nt, dm.reach, dm.S, dm.R,
    )
    group = QH // KH
    span = (reach + 1) * T
    KV = KH * H
    inv_root = 1.0 / math.sqrt(H)
    dp, z, t = lax.axis_index("dp"), lax.axis_index("ctx"), lax.axis_index("tensor")
    zz = n - 1 - z

    barrier = pltpu.get_barrier_semaphore()
    for j in range(1, nt):
        pl.semaphore_signal(barrier, inc=1, device_id={"tensor": t ^ j}, device_id_type=MESH)
    for e in range(2):
        for d in range(n):
            if e or d:
                pl.semaphore_signal(
                    barrier,
                    inc=1,
                    device_id={"dp": dp ^ e, "ctx": lax.rem(z + d, n)},
                    device_id_type=MESH,
                )

    loads = [
        (tok_hbm, s.tok), (kw_hbm, s.kw), (vw_hbm, s.vw), (qw_hbm, s.qw), (cot_hbm, s.cot),
        (ow_hbm, s.ow), (dw_hbm, s.dw), (gw_hbm, s.gw), (uw_hbm, s.uw),
    ]
    loads = [pltpu.make_async_copy(a, b, s.load_sem.at[i]) for i, (a, b) in enumerate(loads)]
    for load in loads:
        load.start()
    (l_tok, l_kw, l_vw, l_qw, l_cot, l_ow, l_dw, l_gw, l_uw) = loads

    def scatter_start(k, buf, recv):
        for j in range(1, nt):
            peer = t ^ j
            remote(
                buf.at[pl.ds(pl.multiple_of(peer * S, S), S)], recv.at[j - 1],
                s.pl_s.at[k, j - 1], s.pl_r.at[k, j - 1], tensor=peer,
            ).start()

    def scatter_sum(k, buf, recv, base):
        mine = pl.ds(pl.multiple_of(t * S, S), S)
        for j in range(1, nt):
            remote(
                buf.at[mine], recv.at[j - 1], s.pl_s.at[k, j - 1], s.pl_r.at[k, j - 1], tensor=t ^ j
            ).wait()
        total = base + buf[mine, :].astype(F32)
        for j in range(1, nt):
            total = total + recv[j - 1].astype(F32)
        return total

    def gather_start(k, full):
        mine = pl.ds(pl.multiple_of(t * S, S), S)
        for j in range(1, nt):
            remote(
                full.at[mine], full.at[mine], s.pl_s.at[k, j - 1], s.pl_r.at[k, j - 1], tensor=t ^ j
            ).start()

    def gather_wait(k, full):
        mine = pl.ds(pl.multiple_of(t * S, S), S)
        for j in range(1, nt):
            peer = t ^ j
            theirs = pl.ds(pl.multiple_of(peer * S, S), S)
            copy = remote(
                full.at[mine], full.at[theirs], s.pl_s.at[k, j - 1], s.pl_r.at[k, j - 1], tensor=peer
            )
            copy.wait_send()
            copy.wait_recv()

    mine = pl.ds(pl.multiple_of(t * S, S), S)

    def spread_start(k, share, full, own):
        own_copy(share, full, own).start()
        for j in range(1, nt):
            remote(
                share, full.at[mine], s.pl_s.at[k, j - 1], s.pl_r.at[k, j - 1], tensor=t ^ j
            ).start()

    def own_copy(share, full, own):
        return pltpu.make_async_copy(share, full.at[mine], s.load_sem.at[own])

    def spread_wait(k, share, full, own):
        own_copy(share, full, own).wait()
        for j in range(1, nt):
            peer = t ^ j
            theirs = pl.ds(pl.multiple_of(peer * S, S), S)
            copy = remote(share, full.at[theirs], s.pl_s.at[k, j - 1], s.pl_r.at[k, j - 1], tensor=peer)
            copy.wait_send()
            copy.wait_recv()

    def line_copy(k, all_ref, up, step, src=None):
        idx = (z - step) if up else (z + step)
        ref = all_ref.at[dp, idx]
        return remote(
            ref if src is None else src, ref,
            s.ag_s.at[k, 0 if up else 1, step], s.ag_r.at[k, 0 if up else 1, step],
            ctx=(z + 1) if up else (z - 1),
        )

    def core_copy(k, all_ref, slot, idx, src=None):
        ref = all_ref.at[dp, idx]
        return remote(
            ref if src is None else src, ref, s.agx_s.at[k, slot], s.agx_r.at[k, slot], dp=1 - dp
        )

    def gather_line_start(k, src, all_ref):
        pltpu.make_async_copy(src, all_ref.at[dp, z], s.own_sem.at[k]).start()

        @pl.when(z < n - 1)
        def _():
            line_copy(k, all_ref, True, 0, src).start()

        @pl.when(z > 0)
        def _():
            line_copy(k, all_ref, False, 0, src).start()

        core_copy(k, all_ref, 0, z, src).start()

    def gather_line_step(k, all_ref, step):
        @pl.when(z >= step)
        def _():
            ref = all_ref.at[dp, z - step]
            remote(ref, ref, s.ag_s.at[k, 0, step - 1], s.ag_r.at[k, 0, step - 1], ctx=z - 1).wait_recv()
            if step < n - 1:

                @pl.when(z < n - 1)
                def _():
                    line_copy(k, all_ref, True, step).start()

            core_copy(k, all_ref, step, z - step).start()

        @pl.when(zz >= step)
        def _():
            ref = all_ref.at[dp, z + step]
            remote(ref, ref, s.ag_s.at[k, 1, step - 1], s.ag_r.at[k, 1, step - 1], ctx=z + 1).wait_recv()
            if step < n - 1:

                @pl.when(z > 0)
                def _():
                    line_copy(k, all_ref, False, step).start()

            core_copy(k, all_ref, n - 1 + step, z + step).start()

    def gather_line_finish(k, src, all_ref):
        pltpu.make_async_copy(src, all_ref.at[dp, z], s.own_sem.at[k]).wait()
        for step in range(n - 1):

            @pl.when((z >= step) & (z < n - 1))
            def _():
                line_copy(k, all_ref, True, step, src).wait_send()

            @pl.when((zz >= step) & (z > 0))
            def _():
                line_copy(k, all_ref, False, step, src).wait_send()

        def both(slot, idx):
            ref = all_ref.at[1 - dp, idx]
            copy = remote(src, ref, s.agx_s.at[k, slot], s.agx_r.at[k, slot], dp=1 - dp)
            copy.wait_send()
            copy.wait_recv()

        both(0, z)
        for step in range(1, n):

            @pl.when(z >= step)
            def _():
                both(step, z - step)

            @pl.when(zz >= step)
            def _():
                both(n - 1 + step, z + step)

    def columns_copy(k, src, all_ref, e, d):
        to_dp, to_z = dp ^ e, lax.rem(z + d, n)
        rows = pl.ds(pl.multiple_of((to_dp * n + to_z) * R, R), R)
        return remote(
            src.at[rows], all_ref.at[dp, z], s.aa_s.at[k, e * n + d], s.aa_r.at[k, e * n + d],
            dp=to_dp, ctx=to_z,
        )

    def columns_own(k, src, all_ref):
        rows = pl.ds(pl.multiple_of((dp * n + z) * R, R), R)
        return pltpu.make_async_copy(src.at[rows], all_ref.at[dp, z], s.aa_s.at[k, 0])

    def columns_start(k, src, all_ref):
        columns_own(k, src, all_ref).start()
        for d in range(n):
            for e in range(2):
                if e or d:
                    columns_copy(k, src, all_ref, e, d).start()

    def columns_wait_send(k, src, all_ref):
        columns_own(k, src, all_ref).wait()
        for e in range(2):
            for d in range(n):
                if e or d:
                    columns_copy(k, src, all_ref, e, d).wait_send()

    def columns_wait_recv(k, src, all_ref):
        for e in range(2):
            for d in range(n):
                if e or d:
                    ref = all_ref.at[dp ^ e, lax.rem(z - d + n, n)]
                    remote(
                        src.at[pl.ds(0, R)], ref, s.aa_s.at[k, e * n + d], s.aa_r.at[k, e * n + d], dp=dp ^ e
                    ).wait_recv()

    def job_dp_start(job, k, b):
        slot = job.dp_slot(b)

        def body(c, w):
            slot[:, pl.ds(c, w)] = job.part((1 - dp) * n + b, c, w).astype(BF16)

        tiles(job.cols, 512, body)
        remote(slot, job.dp_recv(b), s.dp_s.at[k, b], s.dp_r.at[k, b], dp=1 - dp).start()

    def job_dp_wait_send(job, k, b):
        remote(job.dp_slot(b), job.dp_recv(b), s.dp_s.at[k, b], s.dp_r.at[k, b], dp=1 - dp).wait_send()

    def job_dp_wait_all(job, k):
        for b in range(n):
            remote(job.dp_slot(b), job.dp_recv(b), s.dp_s.at[k, b], s.dp_r.at[k, b], dp=1 - dp).wait_recv()

    def chain_copy(job, k, up, step):
        i = 0 if up else 1
        return remote(
            job.chain_slot(up, step), job.chain(up, step), s.ch_s.at[k, i, step], s.ch_r.at[k, i, step],
            ctx=(z + 1) if up else (z - 1),
        )

    def chain_step(job, k, step):
        for up in (True, False):
            pos = z if up else zz

            @pl.when((pos <= step) & (pos < n - 1))
            def _(up=up, pos=pos):
                target = (z + n - 1 - step) if up else (z - (n - 1 - step))
                slot = job.chain_slot(up, step)
                if step:

                    @pl.when(pos >= 1)
                    def _():
                        chain_copy(job, k, up, step - 1).wait_recv()

                def body(c, w):
                    cs = pl.ds(c, w)
                    total = job.part(dp * n + target, c, w) + job.dp_recv(target)[:, cs].astype(F32)
                    if step:
                        prev = job.chain(up, step - 1)[:, cs].astype(F32)
                        total = total + jnp.where(pos >= 1, prev, 0.0)
                    slot[:, cs] = total.astype(BF16)

                tiles(job.cols, 512, body)
                chain_copy(job, k, up, step).start()

    def chain_wait_send(job, k, step):
        for up in (True, False):
            pos = z if up else zz

            @pl.when((pos <= step) & (pos < n - 1))
            def _(up=up):
                chain_copy(job, k, up, step).wait_send()

    def chain_final(job, k, out_ref):
        for up in (True, False):
            pos = z if up else zz

            @pl.when(pos >= 1)
            def _(up=up):
                chain_copy(job, k, up, n - 2).wait_recv()

        def body(c, w):
            cs = pl.ds(c, w)
            total = job.part(dp * n + z, c, w) + job.dp_recv(z)[:, cs].astype(F32)
            a = job.chain(True, n - 2)[:, cs].astype(F32)
            b = job.chain(False, n - 2)[:, cs].astype(F32)
            out_ref[:, cs] = total + jnp.where(z >= 1, a, 0.0) + jnp.where(zz >= 1, b, 0.0)

        tiles(job.cols, 512, body)

    l_tok.wait()
    x = s.tok[...].astype(F32)
    scale = lax.rsqrt(jnp.mean(x * x, axis=-1, keepdims=True) + epsilon)
    s.x1[...] = (x * scale * g1[...]).astype(BF16)
    s.tokshare[...] = s.tok[mine, :].astype(F32)

    def rms(v):
        return lax.rsqrt(jnp.mean(v * v, axis=-1, keepdims=True) + epsilon)

    def rope(v):
        return v * cos[...] + pltpu.roll(v, H // 2, 1) * sin[...]

    def rope_back(g):
        return g * cos[...] + pltpu.roll(g * sin[...], H // 2, 1)

    own_rows = pl.ds(reach * T, T)
    l_kw.wait()
    l_vw.wait()
    s.k_raw[...] = dot(s.x1[...], s.kw[...])
    s.kv[own_rows, KV : 2 * KV] = dot(s.x1[...], s.vw[...]).astype(BF16)
    for h in range(KH):
        raw = s.k_raw[:, h * H : (h + 1) * H]
        s.kv[own_rows, h * H : (h + 1) * H] = rope(raw * rms(raw) * gk[...]).astype(BF16)
    pl.semaphore_wait(barrier, (nt - 1) + (2 * n - 1))

    def kv_copy(r):
        return remote(
            s.kv.at[pl.ds((reach - r + 1) * T, T)], s.kv.at[pl.ds((reach - r) * T, T)],
            s.kv_s.at[r - 1], s.kv_r.at[r - 1], ctx=z + 1,
        )

    def kv_send(r):
        @pl.when((z < n - 1) & (z >= r - 1))
        def _():
            kv_copy(r).start()

    kv_send(1)
    for r in range(1, reach + 1):

        @pl.when(z < r)
        def _():
            s.kv[pl.ds((reach - r) * T, T), :] = jnp.zeros((T, 2 * KV), BF16)

    l_qw.wait()
    s.q_raw[...] = dot(s.x1[...], s.qw[...])
    for h in range(QH):
        raw = s.q_raw[:, h * H : (h + 1) * H]
        s.q_rot[:, h * H : (h + 1) * H] = rope(raw * rms(raw) * gq[...]).astype(BF16)
    for r in range(1, reach + 1):

        @pl.when(z >= r)
        def _():
            kv_copy(r).wait_recv()

        if r < reach:
            kv_send(r + 1)
    rows_i = lax.broadcasted_iota(jnp.int32, (T, span), 0) + reach * T
    cols_i = lax.broadcasted_iota(jnp.int32, (T, span), 1)
    allowed = (cols_i <= rows_i) & (qseg[...] == kseg[...])
    s.mask[...] = jnp.where(allowed, 1.0, 0.0).astype(F32)

    def weights_of(h, g):
        hs = pl.ds(pl.multiple_of(h * H, H), H)
        q = s.q_rot[:, hs]
        k = s.kv[:, pl.ds(pl.multiple_of(g * H, H), H)]
        return q, k, jnp.where(s.mask[...] > 0.0, jnp.exp(dot_nt(q, k) * inv_root), 0.0)

    def attend(h, _):
        g = h // group
        hs = pl.ds(pl.multiple_of(h * H, H), H)
        _q, _k, w = weights_of(h, g)
        v = s.kv[:, pl.ds(pl.multiple_of(KV + g * H, H), H)]
        total = jnp.sum(w, axis=-1, keepdims=True)
        att = dot(w.astype(BF16), v) / total
        s.tot[:, hs] = jnp.broadcast_to(total, (T, H))
        s.att[:, hs] = att
        s.att_low[:, hs] = att.astype(BF16)
        return 0

    lax.fori_loop(0, QH, attend, 0)

    l_ow.wait()

    def body(c, w):
        s.send_a[:, pl.ds(c, w)] = dot(s.att_low[...], s.ow[:, pl.ds(c, w)]).astype(BF16)

    tiles(D, TILE, body)
    scatter_start(0, s.send_a, s.recv0)

    l_cot.wait()
    s.cotshare[...] = s.cot[mine, :].astype(F32)

    def body(c, w):
        s.xt[pl.ds(c, w), :] = s.x1[:, pl.ds(c, w)].astype(F32).T.astype(BF16)
        s.cott[pl.ds(c, w), :] = s.cot[:, pl.ds(c, w)].astype(F32).T.astype(BF16)

    tiles(D, TILE, body)
    columns_start(0, s.cott, cott_all)
    columns_start(1, s.xt, x1t_all)
    l_dw.wait()

    def body(c, w):
        s.gh[:, pl.ds(c, w)] = dot_nt(s.cot[...], s.dw[pl.ds(c, w), :])

    tiles(F, TILE, body)
    for h in range(QH):
        s.attt[h * H : (h + 1) * H, :] = s.att[:, h * H : (h + 1) * H].T.astype(BF16)

    s.resid[...] = scatter_sum(0, s.send_a, s.recv0, s.tokshare[...])
    resid = s.resid[...]
    s.x2[mine, :] = (resid * rms(resid) * g2[...]).astype(BF16)
    gather_start(1, s.x2)
    l_gw.wait()
    l_uw.wait()
    gather_wait(1, s.x2)

    def body(c, w):
        cs = pl.ds(c, w)
        gate = dot(s.x2[...], s.gw[:, cs])
        up = dot(s.x2[...], s.uw[:, cs])
        gh = s.gh[:, cs]
        sig = jax.nn.sigmoid(gate)
        act = gate * sig
        s.hid[:, cs] = (act * up).astype(BF16)
        s.gg[:, cs] = (gh * up * (sig * (1.0 + gate * (1.0 - sig)))).astype(BF16)
        s.gu[:, cs] = (gh * act).astype(BF16)

    tiles(F, TILE, body)
    gather_line_start(0, s.hid, hid_all)

    def body(c, w):
        rs = pl.ds(c, w)
        s.send_a[:, rs] = (
            dot_nt(s.gg[...], s.gw[rs, :]) + dot_nt(s.gu[...], s.uw[rs, :])
        ).astype(BF16)

    tiles(D, TILE, body)
    scatter_start(2, s.send_a, s.recv1)
    pl.semaphore_signal(s.credit, inc=1, device_id={"dp": 1 - dp}, device_id_type=MESH)

    columns_wait_send(1, s.xt, x1t_all)

    def body(c, w):
        s.xt[pl.ds(c, w), :] = s.x2[:, pl.ds(c, w)].astype(F32).T.astype(BF16)

    tiles(D, TILE, body)

    class WeightJob:
        def __init__(self, k, grad):
            self.k, self.grad, self.cols = k, grad, F

        def part(self, block, c, w):
            rows = pl.ds(pl.multiple_of(block * R, R), R)
            return dot(s.xt[rows, :], self.grad[:, pl.ds(c, w)])

        def dp_slot(self, b):
            return s.gw.at[pl.ds(b * R, R)]

        def dp_recv(self, b):
            return s.uw.at[pl.ds(pl.multiple_of((self.k * n + b) * R, R), R)]

        def chain_slot(self, up, step):
            i = (0 if self.k else n) + (step if up else n - 2 - step)
            return s.gw.at[pl.ds(i * R, R)]

        def chain(self, up, step):
            return s.chain.at[self.k, 0 if up else 1, step]

    class OutJob:
        cols = R

        def part(self, block, c, w):
            cs = pl.ds(pl.multiple_of(block * R + c, 128), w)
            return dot(s.attt[...], s.gm[:, cs])

        def dp_slot(self, b):
            return s.cott.at[pl.ds(b * QH * H, QH * H), pl.ds(0, R)]

        def dp_recv(self, b):
            return s.o_recv.at[b]

        def chain_slot(self, up, step):
            return s.o_csend.at[step if up else n - 2 - step]

        def chain(self, up, step):
            return s.o_chain.at[0 if up else 1, step]

    gate_job, up_job, out_job = WeightJob(0, s.gg), WeightJob(1, s.gu), OutJob()
    order = [b for i in range((n + 1) // 2) for b in dict.fromkeys((n - 1 - i, i))]

    pl.semaphore_wait(s.credit, 1)
    for b in order:
        job_dp_start(gate_job, 0, b)

    def body(c, w):
        s.send_b[:, pl.ds(c, w)] = dot(s.hid[...], s.dw[:, pl.ds(c, w)]).astype(BF16)

    tiles(D, TILE, body)
    scatter_start(3, s.send_b, s.recv2)
    for b in order:
        job_dp_wait_send(gate_job, 0, b)
        job_dp_start(up_job, 1, b)
    gather_line_step(0, hid_all, 1)

    grad_second = scatter_sum(2, s.send_a, s.recv1, jnp.zeros((S, D), F32))
    resid = s.resid[...]
    scale = rms(resid)
    normed = resid * scale
    s.gains[:, D : 2 * D] = jnp.sum(grad_second * normed, axis=0, keepdims=True)
    scaled = grad_second * g2[...]
    inner = jnp.mean(scaled * normed, axis=-1, keepdims=True)
    s.gresid[...] = s.cotshare[...] + scale * (scaled - normed * inner)
    s.gm[mine, :] = s.gresid[...].astype(BF16)
    gather_start(4, s.gm)
    job_dp_wait_all(gate_job, 0)
    chain_step(gate_job, 0, 0)
    s.outsh[...] = scatter_sum(3, s.send_b, s.recv2, s.resid[...]).astype(BF16)
    gather_wait(4, s.gm)
    spread_start(5, s.outsh, out_hbm, 0)

    def body(c, w):
        s.gatt[:, pl.ds(c, w)] = dot_nt(s.gm[...], s.ow[pl.ds(c, w), :])

    tiles(QH * H, TILE, body)
    s.gq_acc[...] = jnp.zeros((1, H), F32)

    def back(g, _):
        ks = pl.ds(pl.multiple_of(g * H, H), H)
        vs = pl.ds(pl.multiple_of(KV + g * H, H), H)
        v = s.kv[:, vs]
        grad_k = jnp.zeros((span, H), F32)
        grad_v = jnp.zeros((span, H), F32)
        for i in range(group):
            h = g * group + i
            hs = pl.ds(pl.multiple_of(h * H, H), H)
            q, k, w = weights_of(h, g)
            ga, total = s.gatt[:, hs], s.tot[:, hs]
            gs = (ga / total).astype(BF16)
            delta = jnp.sum(ga * s.att[:, hs], axis=-1, keepdims=True) / total[:, :1]
            ds = (w * (dot_nt(gs, v) - delta)).astype(BF16)
            grad_k = grad_k + dot_tn(ds, q) * inv_root
            grad_v = grad_v + dot_tn(w.astype(BF16), gs)
            gr = rope_back(dot(ds, k) * inv_root)
            raw = s.q_raw[:, hs]
            r = rms(raw)
            nq = raw * r
            s.gq_acc[...] += jnp.sum(gr * nq, axis=0, keepdims=True)
            sc = gr * gq[...]
            s.dqkv[:, hs] = (r * (sc - nq * jnp.mean(sc * nq, axis=-1, keepdims=True))).astype(BF16)
        s.dkv[:, ks] = grad_k.astype(BF16)
        s.dkv[:, vs] = grad_v.astype(BF16)
        return 0

    lax.fori_loop(0, KH, back, 0)
    s.gains[:, 2 * D : 2 * D + H] = s.gq_acc[...]

    def dkv_copy(i):
        return remote(
            s.dkv.at[pl.ds(i * T, T)], s.dkv_in.at[i], s.dkv_s.at[i], s.dkv_r.at[i], ctx=z - 1
        )

    for i in range(reach):
        if i:

            @pl.when((z < n - 1) & (z + 1 >= reach - i + 1))
            def _():
                dkv_copy(i - 1).wait_recv()
                rows = pl.ds(i * T, T)
                s.dkv[rows, :] = (s.dkv[rows, :].astype(F32) + s.dkv_in[i - 1].astype(F32)).astype(BF16)

        @pl.when(z >= reach - i)
        def _():
            dkv_copy(i).start()

        if i == 0:
            job_dp_wait_all(up_job, 1)
            gather_line_step(0, hid_all, 2)
            columns_wait_send(0, s.cott, cott_all)
            for b in order:
                job_dp_start(out_job, 2, b)
            for b in order:
                job_dp_wait_send(up_job, 1, b)
            chain_step(gate_job, 0, 1)

    def last_block():
        rows = pl.ds(reach * T, T)
        own = s.dkv[rows, :].astype(F32)
        extra = s.dkv_in[reach - 1].astype(F32)
        return own + jnp.where(z < n - 1, extra, 0.0)

    @pl.when(z < n - 1)
    def _():
        dkv_copy(reach - 1).wait_recv()

    own = last_block()
    s.dqkv[:, QH * H + KV :] = own[:, KV:].astype(BF16)
    gk_sum = jnp.zeros((1, H), F32)
    for h in range(KH):
        gr = rope_back(own[:, h * H : (h + 1) * H])
        raw = s.k_raw[:, h * H : (h + 1) * H]
        r = rms(raw)
        nk = raw * r
        gk_sum = gk_sum + jnp.sum(gr * nk, axis=0, keepdims=True)
        sc = gr * gk[...]
        s.dqkv[:, QH * H + h * H : QH * H + (h + 1) * H] = (
            r * (sc - nk * jnp.mean(sc * nk, axis=-1, keepdims=True))
        ).astype(BF16)
    s.gains[:, 2 * D + H :] = gk_sum
    gather_line_start(1, s.dqkv, qkv_all)

    q_c, k_c, v_c = pl.ds(0, QH * H), pl.ds(QH * H, KV), pl.ds(QH * H + KV, KV)

    def body(c, w):
        rs = pl.ds(c, w)
        s.send_a[:, rs] = (
            dot_nt(s.dqkv[:, q_c], s.qw[rs, :])
            + dot_nt(s.dqkv[:, k_c], s.kw[rs, :])
            + dot_nt(s.dqkv[:, v_c], s.vw[rs, :])
        ).astype(BF16)

    tiles(D, TILE, body)
    scatter_start(6, s.send_a, s.recv3)
    job_dp_wait_all(out_job, 2)
    chain_step(out_job, 2, 0)
    chain_step(gate_job, 0, 2)
    grad_first = scatter_sum(6, s.send_a, s.recv3, jnp.zeros((S, D), F32))
    tokshare = s.tokshare[...]
    scale = rms(tokshare)
    normed = tokshare * scale
    s.gains[:, :D] = jnp.sum(grad_first * normed, axis=0, keepdims=True)
    scaled = grad_first * g1[...]
    inner = jnp.mean(scaled * normed, axis=-1, keepdims=True)
    s.tgsh[...] = (s.gresid[...] + scale * (scaled - normed * inner)).astype(BF16)
    spread_start(7, s.tgsh, tgrad_hbm, 1)
    for j in range(1, nt):
        remote(s.gains, s.gains_p.at[j - 1], s.pl_s.at[8, j - 1], s.pl_r.at[8, j - 1], tensor=t ^ j).start()
    for step in range(3, n):
        gather_line_step(0, hid_all, step)
    for step in range(3, n - 1):
        chain_step(gate_job, 0, step)
    chain_step(up_job, 1, 0)
    for j in range(1, nt):
        remote(s.gains, s.gains_p.at[j - 1], s.pl_s.at[8, j - 1], s.pl_r.at[8, j - 1], tensor=t ^ j).wait()
    total = s.gains[...]
    for j in range(1, nt):
        total = total + s.gains_p[j - 1]
    s.gains2[...] = total

    def gain_copy(e, d):
        i = e * n + d
        return remote(
            s.gains2, s.gains_x.at[i - 1], s.ga_s.at[i], s.ga_r.at[i], dp=dp ^ e, ctx=lax.rem(z + d, n)
        )

    for e in range(2):
        for d in range(n):
            if e or d:
                gain_copy(e, d).start()
    for step in range(1, n - 1):
        gather_line_step(1, qkv_all, step)
        chain_step(out_job, 2, step)
        chain_step(up_job, 1, step)
    def gate_copy():
        return pltpu.make_async_copy(s.gh.at[pl.ds(0, R)], gate_out, s.load_sem.at[2])

    def up_copy():
        return pltpu.make_async_copy(s.gh.at[pl.ds(0, R)], up_out, s.load_sem.at[3])

    chain_final(gate_job, 0, s.gh.at[pl.ds(0, R)])
    gate_copy().start()
    chain_final(out_job, 2, outw_out)
    gather_line_step(1, qkv_all, n - 1)
    gate_copy().wait()
    chain_final(up_job, 1, s.gh.at[pl.ds(0, R)])
    up_copy().start()
    for e in range(2):
        for d in range(n):
            if e or d:
                gain_copy(e, d).wait()
    total = s.gains2[...]
    for i in range(2 * n - 1):
        total = total + s.gains_x[i]
    gains_out[...] = total

    gather_line_finish(0, s.hid, hid_all)
    gather_line_finish(1, s.dqkv, qkv_all)
    columns_wait_recv(0, s.cott, cott_all)
    columns_wait_recv(1, s.xt, x1t_all)
    for b in range(n):
        job_dp_wait_send(out_job, 2, b)
    for st in range(n - 1):
        chain_wait_send(gate_job, 0, st)
        chain_wait_send(up_job, 1, st)
        chain_wait_send(out_job, 2, st)
    for r in range(1, reach + 1):

        @pl.when((z < n - 1) & (z >= r - 1))
        def _():
            kv_copy(r).wait_send()

    for i in range(reach):

        @pl.when(z >= reach - i)
        def _():
            dkv_copy(i).wait_send()

    spread_wait(5, s.outsh, out_hbm, 0)
    spread_wait(7, s.tgsh, tgrad_hbm, 1)
    up_copy().wait()


def run_layer(dm, *operands):
    T, D, H, F, n, nt, reach, S, R = dm.T, dm.D, dm.H, dm.F, dm.n, dm.nt, dm.reach, dm.S, dm.R
    QC, KV = dm.QH * H, dm.KH * H
    span = (reach + 1) * T
    G = 2 * D + 2 * H
    dma = pltpu.SemaphoreType.DMA
    scratch = dict(
        tok=((T, D), BF16), x1=((T, D), BF16), cot=((T, D), BF16), x2=((T, D), BF16), gm=((T, D), BF16),
        outsh=((S, D), BF16), tgsh=((S, D), BF16), xt=((D, T), BF16), cott=((D, T), BF16),
        qw=((D, QC), BF16), kw=((D, KV), BF16), vw=((D, KV), BF16), ow=((QC, D), BF16),
        gw=((D, F), BF16), uw=((D, F), BF16), dw=((F, D), BF16),
        tokshare=((S, D), F32), cotshare=((S, D), F32), resid=((S, D), F32), gresid=((S, D), F32),
        k_raw=((T, KV), F32), q_raw=((T, QC), F32), q_rot=((T, QC), BF16), kv=((span, 2 * KV), BF16),
        mask=((T, span), F32), tot=((T, QC), F32), att=((T, QC), F32), att_low=((T, QC), BF16),
        attt=((QC, T), BF16), gatt=((T, QC), F32), gq_acc=((1, H), F32),
        recv0=((nt - 1, S, D), BF16), recv1=((nt - 1, S, D), BF16),
        gh=((T, F), F32), hid=((T, F), BF16), gg=((T, F), BF16), gu=((T, F), BF16),
        dkv=((span, 2 * KV), BF16), dkv_in=((reach, T, 2 * KV), BF16), dqkv=((T, QC + 2 * KV), BF16),
        chain=((2, 2, n - 1, R, F), BF16),
        o_recv=((n, QC, R), BF16), o_csend=((n - 1, QC, R), BF16),
        o_chain=((2, n - 1, QC, R), BF16),
        gains=((1, G), F32), gains2=((1, G), F32), gains_p=((nt - 1, 1, G), F32),
        gains_x=((2 * n - 1, 1, G), F32),
    )
    sems = dict(
        load_sem=(9,), own_sem=(2,), pl_s=(9, nt - 1), pl_r=(9, nt - 1), ag_s=(2, 2, n - 1), ag_r=(2, 2, n - 1),
        agx_s=(2, 2 * n - 1), agx_r=(2, 2 * n - 1), aa_s=(2, 2 * n), aa_r=(2, 2 * n),
        dp_s=(3, n), dp_r=(3, n), ch_s=(3, 2, n - 1), ch_r=(3, 2, n - 1), kv_s=(reach,), kv_r=(reach,),
        dkv_s=(reach,), dkv_r=(reach,), ga_s=(2 * n,), ga_r=(2 * n,),
    )
    names = list(scratch) + list(sems) + ["credit"]
    shapes = [pltpu.VMEM(*v) for v in scratch.values()] + [dma(v) for v in sems.values()]
    shapes.append(pltpu.SemaphoreType.REGULAR)

    def body(*refs):
        fixed = len(refs) - len(names)
        s = Dims()
        for name, ref in zip(names, refs[fixed:]):
            setattr(s, name, ref)
        for alias, of in dm.alias.items():
            setattr(s, alias, getattr(s, of))
        layer_kernel(dm, *refs[:fixed], s)

    hbm = pl.BlockSpec(memory_space=pl.ANY)
    vmem = pl.BlockSpec(memory_space=pltpu.VMEM)
    return pl.pallas_call(
        body,
        out_shape=(
            jax.ShapeDtypeStruct((T, D), BF16),
            jax.ShapeDtypeStruct((T, D), BF16),
            jax.ShapeDtypeStruct((R, F), F32),
            jax.ShapeDtypeStruct((R, F), F32),
            jax.ShapeDtypeStruct((QC, R), F32),
            jax.ShapeDtypeStruct((2, n, T, F), BF16),
            jax.ShapeDtypeStruct((2, n, T, QC + 2 * KV), BF16),
            jax.ShapeDtypeStruct((2, n, R, T), BF16),
            jax.ShapeDtypeStruct((2, n, R, T), BF16),
            jax.ShapeDtypeStruct((1, G), F32),
        ),
        in_specs=[hbm] * 2 + [vmem] * 8 + [hbm] * 7,
        out_specs=[hbm] * 4 + [vmem] + [hbm] * 4 + [vmem],
        scratch_shapes=shapes,
        compiler_params=pltpu.CompilerParams(
            collective_id=0, has_side_effects=True, vmem_limit_bytes=67043328
        ),
        name="layer",
    )(*operands)


def per_device(
    tokens,
    segments,
    first_gain,
    query_weight,
    key_matrix,
    value_matrix,
    query_norm_gain,
    key_gain,
    output_weight,
    second_gain,
    gate_weight,
    up_weight,
    down_weight,
    cotangent,
):
    _, T, D = tokens.shape
    dm = Dims()
    dm.T, dm.D, dm.H, dm.F = T, D, query_norm_gain.shape[0], gate_weight.shape[1]
    dm.QH, dm.KH = query_weight.shape[1] // dm.H, key_matrix.shape[1] // dm.H
    dm.n, dm.nt = lax.axis_size("ctx"), lax.axis_size("tensor")
    length = segments.shape[1]
    dm.reach = -(-(length // 2 - 1) // T)
    dm.S, dm.R = T // dm.nt, D // (2 * dm.n)
    dm.alias = {"send_b": "x1", "send_a": "tok", "recv2": "recv0", "recv3": "recv1"}
    H = dm.H
    start = lax.axis_index("ctx") * T
    row = segments[0]
    mine = lax.dynamic_slice_in_dim(row, start, T, 0)
    begins = jnp.sum((row[None, :] < mine[:, None]).astype(jnp.int32), axis=1)
    position = (start + jnp.arange(T, dtype=jnp.int32) - begins).astype(F32)
    inverse = 1.0 / rope_base ** (jnp.arange(0, H, 2, dtype=F32) / H)
    angles = position[:, None] * inverse[None, :]
    cosine, sine = jnp.cos(angles), jnp.sin(angles)
    cosine = jnp.concatenate([cosine, cosine], axis=-1)
    sine = jnp.concatenate([-sine, sine], axis=-1)
    padded = jnp.concatenate([jnp.full((dm.reach * T,), -1, jnp.int32), row])
    keys = lax.dynamic_slice_in_dim(padded, start, (dm.reach + 1) * T, 0)

    out, tgrad, gate_g, up_g, out_g, hid, qkv, x1t, cott, gains = run_layer(
        dm,
        tokens.reshape(T, D),
        cotangent.reshape(T, D),
        first_gain.astype(F32)[None],
        second_gain.astype(F32)[None],
        query_norm_gain.astype(F32)[None],
        key_gain.astype(F32)[None],
        cosine,
        sine,
        mine[:, None],
        keys[None],
        query_weight,
        key_matrix,
        value_matrix,
        output_weight,
        gate_weight,
        up_weight,
        down_weight,
    )

    down_g = jnp.einsum("abtf,abct->fc", hid, cott, preferred_element_type=F32)
    qkv_g = jnp.einsum("abct,abtm->cm", x1t, qkv, preferred_element_type=F32)
    QC, KV = dm.QH * H, dm.KH * H
    gains = gains[0]
    return (
        out.reshape(tokens.shape),
        tgrad.reshape(tokens.shape),
        gains[:D],
        qkv_g[:, :QC],
        qkv_g[:, QC : QC + KV],
        qkv_g[:, QC + KV :],
        gains[2 * D : 2 * D + H],
        gains[2 * D + H :],
        out_g,
        gains[D : 2 * D],
        gate_g,
        up_g,
        down_g,
    )


def solution(mesh):
    return jax.shard_map(
        per_device,
        mesh=mesh,
        in_specs=(
            P("dp", "ctx", None),
            P("dp", None),
            P(),
            P(None, "tensor"),
            P(None, "tensor"),
            P(None, "tensor"),
            P(),
            P(),
            P("tensor", None),
            P(),
            P(None, "tensor"),
            P(None, "tensor"),
            P("tensor", None),
            P("dp", "ctx", None),
        ),
        out_specs=(
            P("dp", "ctx", None),
            P("dp", "ctx", None),
            P(),
            P(("dp", "ctx"), "tensor"),
            P(("dp", "ctx"), "tensor"),
            P(("dp", "ctx"), "tensor"),
            P(),
            P(),
            P("tensor", ("dp", "ctx")),
            P(),
            P(("dp", "ctx"), "tensor"),
            P(("dp", "ctx"), "tensor"),
            P("tensor", ("dp", "ctx")),
        ),
        check_vma=False,
    )
```

profile of v0, /device:TPU:0, one launch (start us, length us, event | category | flops | bytes accessed | tf_op | source)
XLA Modules:
  0.0 249.2 jit_solution(15843344054065160934)
XLA Ops:
  0.7 0.7 fusion.7
  1.4 0.7 constant_dynamic-slice_fusion
  2.0 0.9 convert_reduce_fusion
  3.0 1.2 bitcast_convert_fusion
  4.2 0.8 pad_dynamic-slice_fusion
  4.9 0.6 broadcast_in_dim.39.refs_9_
  5.5 1.3 broadcast_in_dim.40
  6.8 1.3 broadcast_in_dim.41
  8.1 0.8 copy.30.refs_8_
  8.9 0.5 fusion
  9.4 0.8 pad_maximum_fusion
  10.3 222.8 %layer.1 = (bf16[256,2048]{1,0:T(8,128)(2,1)}, bf16[256,2048]{1,0:T(8,128)(2,1)}, f32[256,1536]{1,0:T(8,128)}, f32[256,1536]{1,0:T(8,128)}, f32[512,256]{1,0:T(8...) custom-call(bf16[256,2048]{1,0:T(8,128)(2,1)} %bitcast.34, ...), custom_call_target="tpu_custom_call" | custom-call | tf_op jit(solution)/shard_map/layer/pallas_call | solution.py:823
  233.1 1.2 slice_bitcast_fusion
  234.3 1.3 fusion.2
  235.6 0.0 copy-start.5
  235.6 0.0 copy-start.6
  235.6 3.9 %convolution_bitcast_fusion.1 = f32[256,1024]{1,0:T(8,128)S(1)} fusion(bf16[2,4,256,256]{3,2,1,0:T(8,128)(2,1)} %get-tuple-element.26, bf16[2,4,256,1024]{3,2,1,0:T(8,128)(2,1)} %get-tuple-element.27), kind=kOutput, calls=%fused_computation.1 | convolution fusion | flops 1073741824 | bytes 6291456 | tf_op jit(solution)/shard_map/abct,abtm->cm/dot_general | solution.py:908
  239.5 0.8 slice.44
  240.3 0.8 fusion.1
  241.2 0.0 copy-done.5
  241.2 0.0 copy-done.6
  241.2 0.0 copy-start.3
  241.2 0.0 copy-start.2
  241.2 3.0 %convolution_bitcast_fusion = f32[1536,256]{1,0:T(8,128)} fusion(bf16[2,4,256,1536]{3,2,1,0:T(8,128)(2,1)S(1)} %copy-done.5, bf16[2,4,256,256]{3,2,1,0:T(8,128)(2,1)S(1)} %copy-done.6), kind=kOutput, calls=%fused_computation | convolution fusion | flops 1610612736 | bytes 8912896 | tf_op jit(solution)/shard_map/abtf,abct->fc/dot_general | solution.py:907
  244.2 0.0 copy-done.3
  244.2 0.0 copy-start.4
  244.2 0.0 copy-start.1
  244.2 0.0 copy-start
  244.2 1.0 copy.40
  245.2 0.0 copy-done.2
  245.2 1.0 copy.41
  246.1 0.0 copy-done.4
  246.1 0.8 copy.42
  246.9 0.0 copy-done.1
  246.9 1.1 copy.43
  248.1 0.0 copy-done
  248.1 1.1 copy.44
  (2 shorter events, 0.0 us)
Async XLA Ops:
  235.6 5.6 %copy-start.5 = (bf16[2,4,256,1536]{3,2,1,0:T(8,128)(2,1)S(1)}, bf16[2,4,256,1536]{3,2,1,0:T(8,128)(2,1)}, u32[]{:S(2)}) copy-start(bf16[2,4,256,1536]{3,2,1,0:T(8,128)(2,1)} %get-tuple-element.31) | copy-start | bytes 18874372
  235.6 5.6 %copy-start.6 = (bf16[2,4,256,256]{3,2,1,0:T(8,128)(2,1)S(1)}, bf16[2,4,256,256]{3,2,1,0:T(8,128)(2,1)}, u32[]{:S(2)}) copy-start(bf16[2,4,256,256]{3,2,1,0:T(8,128)(2,1)} %get-tuple-element.32) | copy-start | bytes 3145732
  241.2 3.0 %copy-start.3 = (bf16[256,2048]{1,0:T(8,128)(2,1)S(1)}, bf16[256,2048]{1,0:T(8,128)(2,1)}, u32[]{:S(2)}) copy-start(bf16[256,2048]{1,0:T(8,128)(2,1)} %get-tuple-element.23) | copy-start | bytes 3145732
  241.2 4.0 %copy-start.2 = (bf16[256,2048]{1,0:T(8,128)(2,1)S(1)}, bf16[256,2048]{1,0:T(8,128)(2,1)}, u32[]{:S(2)}) copy-start(bf16[256,2048]{1,0:T(8,128)(2,1)} %get-tuple-element.24) | copy-start | bytes 3145732
  244.2 2.0 copy-start.4
  244.2 2.8 %copy-start.1 = (f32[256,1536]{1,0:T(8,128)S(1)}, f32[256,1536]{1,0:T(8,128)}, u32[]{:S(2)}) copy-start(f32[256,1536]{1,0:T(8,128)} %get-tuple-element.69) | copy-start | bytes 4718596
  244.2 3.9 %copy-start = (f32[256,1536]{1,0:T(8,128)S(1)}, f32[256,1536]{1,0:T(8,128)}, u32[]{:S(2)}) copy-start(f32[256,1536]{1,0:T(8,128)} %get-tuple-element.70) | copy-start | bytes 4718596
where the time goes:
time: 252 us; the launch traced here: 249 us
  Pallas kernels  223 us (88%)
  local copies, waits for them, and re-layouts  12.7 us (5%)
  matrix products  6.88 us (3%)
  other arithmetic  6.08 us (2%)
    pallas_call x1, Pallas kernels, run_layer(): pl.pallas_call(body, out_shape=(jax.ShapeDtypeStruct((T, D), BF16), jax.S...  223 us
    unnamed x19, local copies, waits for them, and re-layouts  5.05 us

commit v1 on v0

--- a/solution.py
+++ b/solution.py
@@ -3,6 +3,7 @@
 
 import jax
 import jax.numpy as jnp
+import numpy as np
 from jax import lax
 from jax.experimental import pallas as pl
 from jax.experimental.pallas import tpu as pltpu
@@ -57,14 +58,9 @@
     dm,
     tok_hbm,
     cot_hbm,
-    g1,
-    g2,
-    gq,
-    gk,
-    cos,
-    sin,
-    qseg,
-    kseg,
+    gain_in,
+    inverse,
+    seg_row,
     qw_hbm,
     kw_hbm,
     vw_hbm,
@@ -76,12 +72,13 @@
     tgrad_hbm,
     gate_out,
     up_out,
+    down_out,
+    q_out,
+    k_out,
+    v_out,
     outw_out,
-    hid_all,
-    qkv_all,
-    x1t_all,
-    cott_all,
     gains_out,
+    att_all,
     s,
 ):
     T, D, H, QH, KH, F, n, nt, reach, S, R = (
@@ -91,8 +88,17 @@
     span = (reach + 1) * T
     KV = KH * H
     inv_root = 1.0 / math.sqrt(H)
+    C = R // nt
+    g1 = gain_in.at[:, pl.ds(0, D)]
+    g2 = gain_in.at[:, pl.ds(D, D)]
+    gq = gain_in.at[:, pl.ds(2 * D, H)]
+    gk = gain_in.at[:, pl.ds(2 * D + H, H)]
+    cos, sin = s.cos, s.sin
     dp, z, t = lax.axis_index("dp"), lax.axis_index("ctx"), lax.axis_index("tensor")
     zz = n - 1 - z
+    nl = n // 2
+    zh, zl = z // nl, lax.rem(z, nl)
+    zzl = nl - 1 - zl
 
     barrier = pltpu.get_barrier_semaphore()
     for j in range(1, nt):
@@ -108,13 +114,13 @@
                 )
 
     loads = [
-        (tok_hbm, s.tok), (kw_hbm, s.kw), (vw_hbm, s.vw), (qw_hbm, s.qw), (cot_hbm, s.cot),
+        (tok_hbm, s.tok), (cot_hbm, s.cot), (kw_hbm, s.kw), (vw_hbm, s.vw), (qw_hbm, s.qw),
         (ow_hbm, s.ow), (dw_hbm, s.dw), (gw_hbm, s.gw), (uw_hbm, s.uw),
     ]
     loads = [pltpu.make_async_copy(a, b, s.load_sem.at[i]) for i, (a, b) in enumerate(loads)]
     for load in loads:
         load.start()
-    (l_tok, l_kw, l_vw, l_qw, l_cot, l_ow, l_dw, l_gw, l_uw) = loads
+    (l_tok, l_cot, l_kw, l_vw, l_qw, l_ow, l_dw, l_gw, l_uw) = loads
 
     def scatter_start(k, buf, recv):
         for j in range(1, nt):
@@ -174,6 +180,20 @@
             copy.wait_send()
             copy.wait_recv()
 
+    def mirror(i, src, dst):
+        return remote(src.at[mine], dst.at[mine], s.mi_s.at[i], s.mi_r.at[i], ctx=zz)
+
+    def mirror_x1(d):
+        cols = pl.ds(pl.multiple_of((d * n + (1 - zh) * nl) * R, 128), nl * R)
+        return remote(
+            s.x1.at[:, cols], s.x1b.at[:, pl.ds(d * nl * R, nl * R)], s.mi_s.at[2 + d], s.mi_r.at[2 + d], ctx=zz
+        )
+
+    def mirror_qkv():
+        return remote(
+            s.dqkv.at[pl.ds(0, T)], s.dqkv.at[pl.ds(T, T)], s.mi_s.at[4], s.mi_r.at[4], ctx=zz
+        )
+
     def line_copy(k, all_ref, up, step, src=None):
         idx = (z - step) if up else (z + step)
         ref = all_ref.at[dp, idx]
@@ -256,17 +276,23 @@
             def _():
                 both(n - 1 + step, z + step)
 
+    me = dp * n + z
+
+    def columns_src(k, src, block):
+        if k < 2:
+            rows = pl.ds(pl.multiple_of(lax.rem(block, n) * R + t * C, C), C)
+            return src.at[rows, pl.ds(pl.multiple_of(block // n * T, T), T)]
+        return src.at[mine, pl.ds(pl.multiple_of(block * R, R), R)]
+
     def columns_copy(k, src, all_ref, e, d):
         to_dp, to_z = dp ^ e, lax.rem(z + d, n)
-        rows = pl.ds(pl.multiple_of((to_dp * n + to_z) * R, R), R)
         return remote(
-            src.at[rows], all_ref.at[dp, z], s.aa_s.at[k, e * n + d], s.aa_r.at[k, e * n + d],
-            dp=to_dp, ctx=to_z,
+            columns_src(k, src, to_dp * n + to_z), all_ref.at[t, me],
+            s.aa_s.at[k, e * n + d], s.aa_r.at[k, e * n + d], dp=to_dp, ctx=to_z,
         )
 
     def columns_own(k, src, all_ref):
-        rows = pl.ds(pl.multiple_of((dp * n + z) * R, R), R)
-        return pltpu.make_async_copy(src.at[rows], all_ref.at[dp, z], s.aa_s.at[k, 0])
+        return pltpu.make_async_copy(columns_src(k, src, me), all_ref.at[t, me], s.aa_s.at[k, 0])
 
     def columns_start(k, src, all_ref):
         columns_own(k, src, all_ref).start()
@@ -276,26 +302,41 @@
                     columns_copy(k, src, all_ref, e, d).start()
 
     def columns_wait_send(k, src, all_ref):
+        for e in range(2):
+            for d in range(n):
+                if e or d:
+                    columns_copy(k, src, all_ref, e, d).wait_send()
+
+    def columns_wait_recv(k, src, all_ref):
         columns_own(k, src, all_ref).wait()
         for e in range(2):
             for d in range(n):
                 if e or d:
-                    columns_copy(k, src, all_ref, e, d).wait_send()
-
-    def columns_wait_recv(k, src, all_ref):
-        for e in range(2):
-            for d in range(n):
-                if e or d:
-                    ref = all_ref.at[dp ^ e, lax.rem(z - d + n, n)]
+                    ref = all_ref.at[t, (dp ^ e) * n + lax.rem(z - d + n, n)]
                     remote(
-                        src.at[pl.ds(0, R)], ref, s.aa_s.at[k, e * n + d], s.aa_r.at[k, e * n + d], dp=dp ^ e
+                        columns_src(k, src, me), ref, s.aa_s.at[k, e * n + d], s.aa_r.at[k, e * n + d],
+                        dp=dp ^ e, ctx=lax.rem(z - d + n, n),
                     ).wait_recv()
+
+    def share_start(k, all_ref):
+        for j in range(1, nt):
+            remote(
+                all_ref.at[t], all_ref.at[t], s.pl_s.at[10 + k, j - 1], s.pl_r.at[10 + k, j - 1], tensor=t ^ j
+            ).start()
+
+    def share_wait(k, all_ref):
+        for j in range(1, nt):
+            copy = remote(
+                all_ref.at[t], all_ref.at[t ^ j], s.pl_s.at[10 + k, j - 1], s.pl_r.at[10 + k, j - 1], tensor=t ^ j
+            )
+            copy.wait_send()
+            copy.wait_recv()
 
     def job_dp_start(job, k, b):
         slot = job.dp_slot(b)
 
         def body(c, w):
-            slot[:, pl.ds(c, w)] = job.part((1 - dp) * n + b, c, w).astype(BF16)
+            slot[:, pl.ds(c, w)] = job.part((1 - dp) * nl + b, c, w).astype(BF16)
 
         tiles(job.cols, 512, body)
         remote(slot, job.dp_recv(b), s.dp_s.at[k, b], s.dp_r.at[k, b], dp=1 - dp).start()
@@ -304,63 +345,71 @@
         remote(job.dp_slot(b), job.dp_recv(b), s.dp_s.at[k, b], s.dp_r.at[k, b], dp=1 - dp).wait_send()
 
     def job_dp_wait_all(job, k):
-        for b in range(n):
+        for b in range(nl):
             remote(job.dp_slot(b), job.dp_recv(b), s.dp_s.at[k, b], s.dp_r.at[k, b], dp=1 - dp).wait_recv()
 
-    def chain_copy(job, k, up, step):
+    def chain_copy(job, k, up, step, part):
         i = 0 if up else 1
+        width = job.cols // 2
+        cols = pl.ds(part * width, width)
         return remote(
-            job.chain_slot(up, step), job.chain(up, step), s.ch_s.at[k, i, step], s.ch_r.at[k, i, step],
+            job.chain_slot(up, step).at[:, cols], job.chain(up, step).at[:, cols],
+            s.ch_s.at[k, i, step, part], s.ch_r.at[k, i, step, part],
             ctx=(z + 1) if up else (z - 1),
         )
 
-    def chain_step(job, k, step):
-        for up in (True, False):
-            pos = z if up else zz
-
-            @pl.when((pos <= step) & (pos < n - 1))
-            def _(up=up, pos=pos):
-                target = (z + n - 1 - step) if up else (z - (n - 1 - step))
-                slot = job.chain_slot(up, step)
-                if step:
-
-                    @pl.when(pos >= 1)
-                    def _():
-                        chain_copy(job, k, up, step - 1).wait_recv()
-
-                def body(c, w):
-                    cs = pl.ds(c, w)
-                    total = job.part(dp * n + target, c, w) + job.dp_recv(target)[:, cs].astype(F32)
+    def chain_step(job, k, step, ways=(True, False), parts=(0, 1)):
+        width = job.cols // 2
+        for part in parts:
+            for up in ways:
+                pos = zl if up else zzl
+
+                @pl.when((pos <= step) & (pos < nl - 1))
+                def _(up=up, pos=pos, part=part):
+                    target = (zl + nl - 1 - step) if up else (zl - (nl - 1 - step))
+                    slot = job.chain_slot(up, step)
                     if step:
-                        prev = job.chain(up, step - 1)[:, cs].astype(F32)
-                        total = total + jnp.where(pos >= 1, prev, 0.0)
-                    slot[:, cs] = total.astype(BF16)
-
-                tiles(job.cols, 512, body)
-                chain_copy(job, k, up, step).start()
+
+                        @pl.when(pos >= 1)
+                        def _():
+                            chain_copy(job, k, up, step - 1, part).wait_recv()
+
+                    def body(c, w):
+                        cs = pl.ds(pl.multiple_of(part * width + c, 128), w)
+                        total = job.part(dp * nl + target, cs.start, w)
+                        total = total + job.dp_recv(target)[:, cs].astype(F32)
+                        if step:
+                            prev = job.chain(up, step - 1)[:, cs].astype(F32)
+                            total = total + jnp.where(pos >= 1, prev, 0.0)
+                        slot[:, cs] = total.astype(BF16)
+
+                    tiles(width, 256 if width % 256 == 0 else 128, body)
+                    chain_copy(job, k, up, step, part).start()
 
     def chain_wait_send(job, k, step):
         for up in (True, False):
-            pos = z if up else zz
-
-            @pl.when((pos <= step) & (pos < n - 1))
+            pos = zl if up else zzl
+
+            @pl.when((pos <= step) & (pos < nl - 1))
             def _(up=up):
-                chain_copy(job, k, up, step).wait_send()
+                for part in range(2):
+                    chain_copy(job, k, up, step, part).wait_send()
 
     def chain_final(job, k, out_ref):
         for up in (True, False):
-            pos = z if up else zz
+            pos = zl if up else zzl
 
             @pl.when(pos >= 1)
             def _(up=up):
-                chain_copy(job, k, up, n - 2).wait_recv()
+                for part in range(2):
+                    chain_copy(job, k, up, nl - 2, part).wait_recv()
 
         def body(c, w):
             cs = pl.ds(c, w)
-            total = job.part(dp * n + z, c, w) + job.dp_recv(z)[:, cs].astype(F32)
-            a = job.chain(True, n - 2)[:, cs].astype(F32)
-            b = job.chain(False, n - 2)[:, cs].astype(F32)
-            out_ref[:, cs] = total + jnp.where(z >= 1, a, 0.0) + jnp.where(zz >= 1, b, 0.0)
+            total = job.part(dp * nl + zl, c, w) + job.dp_recv(zl)[:, cs].astype(F32)
+            a = job.chain(True, nl - 2)[:, cs].astype(F32)
+            b = job.chain(False, nl - 2)[:, cs].astype(F32)
+            out_ref[:, cs] = total + jnp.where(zl >= 1, a, 0.0) + jnp.where(zzl >= 1, b, 0.0)
 
         tiles(job.cols, 512, body)
 
@@ -369,6 +418,9 @@
     scale = lax.rsqrt(jnp.mean(x * x, axis=-1, keepdims=True) + epsilon)
     s.x1[...] = (x * scale * g1[...]).astype(BF16)
     s.tokshare[...] = s.tok[mine, :].astype(F32)
+    l_cot.wait()
+    pl.semaphore_wait(barrier, (nt - 1) + (2 * n - 1))
+    pl.when(zh == 1)(lambda: mirror(0, s.cot, s.cot2).start())
 
     def rms(v):
         return lax.rsqrt(jnp.mean(v * v, axis=-1, keepdims=True) + epsilon)
@@ -378,6 +430,21 @@
 
     def rope_back(g):
         return g * cos[...] + pltpu.roll(g * sin[...], H // 2, 1)
+
+    L = seg_row.shape[1]
+    s.segs[:, : reach * T] = jnp.full((1, reach * T), -1, jnp.int32)
+    s.segs[:, reach * T :] = seg_row[...]
+    row = seg_row[...]
+    at_me = lax.broadcasted_iota(jnp.int32, (T, L), 1) == lax.broadcasted_iota(jnp.int32, (T, L), 0) + z * T
+    row_f = jnp.broadcast_to(row.astype(F32), (T, L))
+    qseg_f = jnp.sum(jnp.where(at_me, row_f, 0.0), axis=1, keepdims=True)
+    begins = jnp.sum(jnp.where(row_f < qseg_f, 1.0, 0.0), axis=1, keepdims=True)
+    position = (lax.broadcasted_iota(jnp.int32, (T, H), 0) + z * T).astype(F32) - begins
+    angles = position * inverse[...]
+    cos[...] = jnp.cos(angles)
+    lane = lax.broadcasted_iota(jnp.int32, (T, H), 1)
+    turned = jnp.sin(angles)
+    sin[...] = jnp.where(lane < H // 2, -turned, turned)
 
     own_rows = pl.ds(reach * T, T)
     l_kw.wait()
@@ -387,7 +454,6 @@
     for h in range(KH):
         raw = s.k_raw[:, h * H : (h + 1) * H]
         s.kv[own_rows, h * H : (h + 1) * H] = rope(raw * rms(raw) * gk[...]).astype(BF16)
-    pl.semaphore_wait(barrier, (nt - 1) + (2 * n - 1))
 
     def kv_copy(r):
         return remote(
@@ -422,7 +488,8 @@
             kv_send(r + 1)
     rows_i = lax.broadcasted_iota(jnp.int32, (T, span), 0) + reach * T
     cols_i = lax.broadcasted_iota(jnp.int32, (T, span), 1)
-    allowed = (cols_i <= rows_i) & (qseg[...] == kseg[...])
+    kseg_f = s.segs[:, pl.ds(pl.multiple_of(z * T, T), span)].astype(F32)
+    allowed = (cols_i <= rows_i) & (qseg_f == kseg_f)
     s.mask[...] = jnp.where(allowed, 1.0, 0.0).astype(F32)
 
     def weights_of(h, g):
@@ -441,6 +508,7 @@
         s.tot[:, hs] = jnp.broadcast_to(total, (T, H))
         s.att[:, hs] = att
         s.att_low[:, hs] = att.astype(BF16)
+        s.attt[hs, :] = att.T.astype(BF16)
         return 0
 
     lax.fori_loop(0, QH, attend, 0)
@@ -453,120 +521,98 @@
     tiles(D, TILE, body)
     scatter_start(0, s.send_a, s.recv0)
 
-    l_cot.wait()
+    def transpose_half(src, dst, place):
+        for d in range(2):
+
+            def body(c, w):
+                cs = pl.ds(pl.multiple_of((d * n + zh * nl) * R + c, 128), w)
+                rows = pl.ds(pl.multiple_of(d * nl * R + c, 128), w)
+                dst[rows, place * T : (place + 1) * T] = src[:, cs].astype(F32).T.astype(BF16)
+
+            tiles(nl * R, TILE, body)
+
     s.cotshare[...] = s.cot[mine, :].astype(F32)
 
-    def body(c, w):
-        s.xt[pl.ds(c, w), :] = s.x1[:, pl.ds(c, w)].astype(F32).T.astype(BF16)
-        s.cott[pl.ds(c, w), :] = s.cot[:, pl.ds(c, w)].astype(F32).T.astype(BF16)
-
-    tiles(D, TILE, body)
-    columns_start(0, s.cott, cott_all)
-    columns_start(1, s.xt, x1t_all)
+    transpose_half(s.x1, s.x1t, 0)
+    transpose_half(s.cot, s.cott, 0)
     l_dw.wait()
 
-    def body(c, w):
-        s.gh[:, pl.ds(c, w)] = dot_nt(s.cot[...], s.dw[pl.ds(c, w), :])
-
-    tiles(F, TILE, body)
-    for h in range(QH):
-        s.attt[h * H : (h + 1) * H, :] = s.att[:, h * H : (h + 1) * H].T.astype(BF16)
+    def hidden_grad(cot, out):
+        def body(c, w):
+            out[:, pl.ds(c, w)] = dot_nt(cot[...], s.dw[pl.ds(c, w), :])
+
+        tiles(F, TILE, body)
+
+    def cot_share():
+        mirror(0, s.cot, s.cot2).wait_recv()
+        gather_start(9, s.cot2)
+
+    hidden_grad(s.cot, s.gh)
 
     s.resid[...] = scatter_sum(0, s.send_a, s.recv0, s.tokshare[...])
     resid = s.resid[...]
     s.x2[mine, :] = (resid * rms(resid) * g2[...]).astype(BF16)
     gather_start(1, s.x2)
+    mirror(1, s.x2, s.x2b).start()
+    pl.when(zh == 0)(lambda: mirror(0, s.cot, s.cot2).start())
+    gather_line_start(2, s.attt, att_all)
     l_gw.wait()
     l_uw.wait()
     gather_wait(1, s.x2)
 
-    def body(c, w):
-        cs = pl.ds(c, w)
-        gate = dot(s.x2[...], s.gw[:, cs])
-        up = dot(s.x2[...], s.uw[:, cs])
-        gh = s.gh[:, cs]
-        sig = jax.nn.sigmoid(gate)
-        act = gate * sig
-        s.hid[:, cs] = (act * up).astype(BF16)
-        s.gg[:, cs] = (gh * up * (sig * (1.0 + gate * (1.0 - sig)))).astype(BF16)
-        s.gu[:, cs] = (gh * act).astype(BF16)
-
-    tiles(F, TILE, body)
-    gather_line_start(0, s.hid, hid_all)
+    def mirrored_share():
+        mirror(1, s.x2, s.x2b).wait_recv()
+        gather_start(10, s.x2b)
+
+    pl.when(zh == 1)(mirrored_share)
+    pl.when(zh == 0)(cot_share)
+
+    def feed(x, grad_hidden, place):
+        rows = pl.ds(place * T, T)
+
+        def body(c, w):
+            cs = pl.ds(c, w)
+            gate = dot(x[...], s.gw[:, cs])
+            up = dot(x[...], s.uw[:, cs])
+            gh = grad_hidden[:, cs]
+            sig = jax.nn.sigmoid(gate)
+            act = gate * sig
+            s.hid[rows, cs] = (act * up).astype(BF16)
+            s.gg[rows, cs] = (gh * up * (sig * (1.0 + gate * (1.0 - sig)))).astype(BF16)
+            s.gu[rows, cs] = (gh * act).astype(BF16)
+
+        tiles(F, TILE, body)
+
+    feed(s.x2, s.gh, 0)
+    pl.when(zh == 0)(mirrored_share)
+    pl.when(zh == 1)(cot_share)
+    for d in range(2):
+        mirror_x1(d).start()
+    own_part = pl.ds(0, T)
 
     def body(c, w):
         rs = pl.ds(c, w)
         s.send_a[:, rs] = (
-            dot_nt(s.gg[...], s.gw[rs, :]) + dot_nt(s.gu[...], s.uw[rs, :])
+            dot_nt(s.gg[own_part, :], s.gw[rs, :]) + dot_nt(s.gu[own_part, :], s.uw[rs, :])
         ).astype(BF16)
 
     tiles(D, TILE, body)
+    transpose_half(s.x2, s.xt, 0)
+    mirror(1, s.x2, s.x2b).wait_send()
     scatter_start(2, s.send_a, s.recv1)
+
+    def body(c, w):
+        s.send_b[:, pl.ds(c, w)] = dot(s.hid[own_part, :], s.dw[:, pl.ds(c, w)]).astype(BF16)
+
+    tiles(D, TILE, body)
+    gather_wait(9, s.cot2)
+    hidden_grad(s.cot2, s.gh2)
+    transpose_half(s.cot2, s.cott, 1)
+    gather_wait(10, s.x2b)
+    feed(s.x2b, s.gh2, 1)
+    transpose_half(s.x2b, s.xt, 1)
+    gather_line_step(2, att_all, 1)
     pl.semaphore_signal(s.credit, inc=1, device_id={"dp": 1 - dp}, device_id_type=MESH)
-
-    columns_wait_send(1, s.xt, x1t_all)
-
-    def body(c, w):
-        s.xt[pl.ds(c, w), :] = s.x2[:, pl.ds(c, w)].astype(F32).T.astype(BF16)
-
-    tiles(D, TILE, body)
-
-    class WeightJob:
-        def __init__(self, k, grad):
-            self.k, self.grad, self.cols = k, grad, F
-
-        def part(self, block, c, w):
-            rows = pl.ds(pl.multiple_of(block * R, R), R)
-            return dot(s.xt[rows, :], self.grad[:, pl.ds(c, w)])
-
-        def dp_slot(self, b):
-            return s.gw.at[pl.ds(b * R, R)]
-
-        def dp_recv(self, b):
-            return s.uw.at[pl.ds(pl.multiple_of((self.k * n + b) * R, R), R)]
-
-        def chain_slot(self, up, step):
-            i = (0 if self.k else n) + (step if up else n - 2 - step)
-            return s.gw.at[pl.ds(i * R, R)]
-
-        def chain(self, up, step):
-            return s.chain.at[self.k, 0 if up else 1, step]
-
-    class OutJob:
-        cols = R
-
-        def part(self, block, c, w):
-            cs = pl.ds(pl.multiple_of(block * R + c, 128), w)
-            return dot(s.attt[...], s.gm[:, cs])
-
-        def dp_slot(self, b):
-            return s.cott.at[pl.ds(b * QH * H, QH * H), pl.ds(0, R)]
-
-        def dp_recv(self, b):
-            return s.o_recv.at[b]
-
-        def chain_slot(self, up, step):
-            return s.o_csend.at[step if up else n - 2 - step]
-
-        def chain(self, up, step):
-            return s.o_chain.at[0 if up else 1, step]
-
-    gate_job, up_job, out_job = WeightJob(0, s.gg), WeightJob(1, s.gu), OutJob()
-    order = [b for i in range((n + 1) // 2) for b in dict.fromkeys((n - 1 - i, i))]
-
-    pl.semaphore_wait(s.credit, 1)
-    for b in order:
-        job_dp_start(gate_job, 0, b)
-
-    def body(c, w):
-        s.send_b[:, pl.ds(c, w)] = dot(s.hid[...], s.dw[:, pl.ds(c, w)]).astype(BF16)
-
-    tiles(D, TILE, body)
-    scatter_start(3, s.send_b, s.recv2)
-    for b in order:
-        job_dp_wait_send(gate_job, 0, b)
-        job_dp_start(up_job, 1, b)
-    gather_line_step(0, hid_all, 1)
 
     grad_second = scatter_sum(2, s.send_a, s.recv1, jnp.zeros((S, D), F32))
     resid = s.resid[...]
@@ -578,14 +624,64 @@
     s.gresid[...] = s.cotshare[...] + scale * (scaled - normed * inner)
     s.gm[mine, :] = s.gresid[...].astype(BF16)
     gather_start(4, s.gm)
-    job_dp_wait_all(gate_job, 0)
-    chain_step(gate_job, 0, 0)
-    s.outsh[...] = scatter_sum(3, s.send_b, s.recv2, s.resid[...]).astype(BF16)
+    columns_start(2, s.gm, s.gmc)
+
+    class WeightJob:
+        def __init__(self, k, left, grad):
+            self.k, self.left, self.grad, self.cols = k, left, grad, grad.shape[1]
+
+        def part(self, block, c, w):
+            rows = pl.ds(pl.multiple_of(block * R, R), R)
+            return dot(self.left[rows, :], self.grad[:, pl.ds(c, w)])
+
+        def dp_slot(self, b):
+            return s.gw.at[pl.ds(b * R, R), pl.ds(0, self.cols)]
+
+        def dp_recv(self, b):
+            return s.uw.at[pl.ds(pl.multiple_of((self.k * nl + b) * R, R), R), pl.ds(0, self.cols)]
+
+        def chain_slot(self, up, step):
+            i = nl + self.k * (nl - 1) + (step if up else nl - 2 - step)
+            return s.gw.at[pl.ds(i * R, R), pl.ds(0, self.cols)]
+
+        def chain(self, up, step):
+            return s.chain.at[self.k, 0 if up or nl == 2 else 1, step, :, pl.ds(0, self.cols)]
+
+    jobs = [
+        WeightJob(0, s.cott, s.hid),
+        WeightJob(1, s.xt, s.gg),
+        WeightJob(2, s.xt, s.gu),
+        WeightJob(3, s.x1t, s.dqkv),
+    ]
+    order = [b for i in range((nl + 1) // 2) for b in dict.fromkeys((nl - 1 - i, i))]
+
+    def job_dp(k):
+        for b in order:
+            if k:
+                job_dp_wait_send(jobs[k - 1], k - 1, b)
+            job_dp_start(jobs[k], k, b)
+
+    pl.semaphore_wait(s.credit, 1)
+    job_dp(0)
+    job_dp_wait_all(jobs[0], 0)
+    chain_step(jobs[0], 0, 0, (True, False), (0,))
+    chain_step(jobs[0], 0, 0, (True,), (1,))
+    job_dp(1)
+    gather_line_step(2, att_all, 2)
     gather_wait(4, s.gm)
-    spread_start(5, s.outsh, out_hbm, 0)
+    scatter_start(3, s.send_b, s.recv2)
+    for d in range(2):
+        mirror_x1(d).wait_recv()
 
     def body(c, w):
-        s.gatt[:, pl.ds(c, w)] = dot_nt(s.gm[...], s.ow[pl.ds(c, w), :])
+        s.x1t[pl.ds(c, w), T : 2 * T] = s.x1b[:, pl.ds(c, w)].astype(F32).T.astype(BF16)
+
+    tiles(D // 2, TILE, body)
+
+    gatt = s.gh.at[:, pl.ds(0, QH * H)]
+
+    def body(c, w):
+        gatt[:, pl.ds(c, w)] = dot_nt(s.gm[...], s.ow[pl.ds(c, w), :])
 
     tiles(QH * H, TILE, body)
     s.gq_acc[...] = jnp.zeros((1, H), F32)
@@ -600,7 +696,7 @@
             h = g * group + i
             hs = pl.ds(pl.multiple_of(h * H, H), H)
             q, k, w = weights_of(h, g)
-            ga, total = s.gatt[:, hs], s.tot[:, hs]
+            ga, total = gatt[:, hs], s.tot[:, hs]
             gs = (ga / total).astype(BF16)
             delta = jnp.sum(ga * s.att[:, hs], axis=-1, keepdims=True) / total[:, :1]
             ds = (w * (dot_nt(gs, v) - delta)).astype(BF16)
@@ -612,7 +708,7 @@
             nq = raw * r
             s.gq_acc[...] += jnp.sum(gr * nq, axis=0, keepdims=True)
             sc = gr * gq[...]
-            s.dqkv[:, hs] = (r * (sc - nq * jnp.mean(sc * nq, axis=-1, keepdims=True))).astype(BF16)
+            s.dqkv[:T, hs] = (r * (sc - nq * jnp.mean(sc * nq, axis=-1, keepdims=True))).astype(BF16)
         s.dkv[:, ks] = grad_k.astype(BF16)
         s.dkv[:, vs] = grad_v.astype(BF16)
         return 0
@@ -639,27 +735,20 @@
             dkv_copy(i).start()
 
         if i == 0:
-            job_dp_wait_all(up_job, 1)
-            gather_line_step(0, hid_all, 2)
-            columns_wait_send(0, s.cott, cott_all)
-            for b in order:
-                job_dp_start(out_job, 2, b)
-            for b in order:
-                job_dp_wait_send(up_job, 1, b)
-            chain_step(gate_job, 0, 1)
-
-    def last_block():
-        rows = pl.ds(reach * T, T)
-        own = s.dkv[rows, :].astype(F32)
-        extra = s.dkv_in[reach - 1].astype(F32)
-        return own + jnp.where(z < n - 1, extra, 0.0)
+            job_dp_wait_all(jobs[1], 1)
+            chain_step(jobs[1], 1, 0, (True,))
+            job_dp(2)
+
+    chain_step(jobs[0], 0, 0, (False,), (1,))
+    chain_step(jobs[1], 1, 0, (False,))
 
     @pl.when(z < n - 1)
     def _():
         dkv_copy(reach - 1).wait_recv()
 
-    own = last_block()
-    s.dqkv[:, QH * H + KV :] = own[:, KV:].astype(BF16)
+    own = s.dkv[pl.ds(reach * T, T), :].astype(F32)
+    own = own + jnp.where(z < n - 1, s.dkv_in[reach - 1].astype(F32), 0.0)
+    s.dqkv[:T, QH * H + KV :] = own[:, KV:].astype(BF16)
     gk_sum = jnp.zeros((1, H), F32)
     for h in range(KH):
         gr = rope_back(own[:, h * H : (h + 1) * H])
@@ -668,27 +757,27 @@
         nk = raw * r
         gk_sum = gk_sum + jnp.sum(gr * nk, axis=0, keepdims=True)
         sc = gr * gk[...]
-        s.dqkv[:, QH * H + h * H : QH * H + (h + 1) * H] = (
+        s.dqkv[:T, QH * H + h * H : QH * H + (h + 1) * H] = (
             r * (sc - nk * jnp.mean(sc * nk, axis=-1, keepdims=True))
         ).astype(BF16)
     s.gains[:, 2 * D + H :] = gk_sum
-    gather_line_start(1, s.dqkv, qkv_all)
+    mirror_qkv().start()
+    job_dp_wait_all(jobs[2], 2)
+    chain_step(jobs[2], 2, 0)
 
     q_c, k_c, v_c = pl.ds(0, QH * H), pl.ds(QH * H, KV), pl.ds(QH * H + KV, KV)
 
     def body(c, w):
         rs = pl.ds(c, w)
         s.send_a[:, rs] = (
-            dot_nt(s.dqkv[:, q_c], s.qw[rs, :])
-            + dot_nt(s.dqkv[:, k_c], s.kw[rs, :])
-            + dot_nt(s.dqkv[:, v_c], s.vw[rs, :])
+            dot_nt(s.dqkv[:T, q_c], s.qw[rs, :])
+            + dot_nt(s.dqkv[:T, k_c], s.kw[rs, :])
+            + dot_nt(s.dqkv[:T, v_c], s.vw[rs, :])
         ).astype(BF16)
 
     tiles(D, TILE, body)
     scatter_start(6, s.send_a, s.recv3)
-    job_dp_wait_all(out_job, 2)
-    chain_step(out_job, 2, 0)
-    chain_step(gate_job, 0, 2)
+    s.outsh[...] = scatter_sum(3, s.send_b, s.recv2, s.resid[...]).astype(BF16)
     grad_first = scatter_sum(6, s.send_a, s.recv3, jnp.zeros((S, D), F32))
     tokshare = s.tokshare[...]
     scale = rms(tokshare)
@@ -700,11 +789,9 @@
     spread_start(7, s.tgsh, tgrad_hbm, 1)
     for j in range(1, nt):
         remote(s.gains, s.gains_p.at[j - 1], s.pl_s.at[8, j - 1], s.pl_r.at[8, j - 1], tensor=t ^ j).start()
-    for step in range(3, n):
-        gather_line_step(0, hid_all, step)
-    for step in range(3, n - 1):
-        chain_step(gate_job, 0, step)
-    chain_step(up_job, 1, 0)
+    columns_wait_recv(2, s.gm, s.gmc)
+    share_start(2, s.gmc)
+    spread_start(5, s.outsh, out_hbm, 0)
     for j in range(1, nt):
         remote(s.gains, s.gains_p.at[j - 1], s.pl_s.at[8, j - 1], s.pl_r.at[8, j - 1], tensor=t ^ j).wait()
     total = s.gains[...]
@@ -722,22 +809,84 @@
         for d in range(n):
             if e or d:
                 gain_copy(e, d).start()
-    for step in range(1, n - 1):
-        gather_line_step(1, qkv_all, step)
-        chain_step(out_job, 2, step)
-        chain_step(up_job, 1, step)
+    mirror_qkv().wait_recv()
+    job_dp(3)
+    job_dp_wait_all(jobs[3], 3)
+    chain_step(jobs[3], 3, 0)
+    for step in range(1, nl - 1):
+        for k, job in enumerate(jobs):
+            chain_step(job, k, step)
+
+    stage = s.gh2.at[pl.ds(0, R), pl.ds(0, QH * H + 2 * KV)]
+
     def gate_copy():
         return pltpu.make_async_copy(s.gh.at[pl.ds(0, R)], gate_out, s.load_sem.at[2])
 
     def up_copy():
         return pltpu.make_async_copy(s.gh.at[pl.ds(0, R)], up_out, s.load_sem.at[3])
 
-    chain_final(gate_job, 0, s.gh.at[pl.ds(0, R)])
+    def qkv_copies():
+        parts = [(q_out, 0, QH * H), (k_out, QH * H, KV), (v_out, QH * H + KV, KV)]
+        return [
+            pltpu.make_async_copy(stage.at[:, pl.ds(a, w)], ref, s.load_sem.at[6 + i])
+            for i, (ref, a, w) in enumerate(parts)
+        ]
+
+    rows = pl.ds(0, R)
+    chain_final(jobs[0], 0, s.gh.at[rows])
+    width = min(256, F)
+    flip = s.gh2.at[:, pl.ds(QH * H + 2 * KV, 2 * R)]
+
+    def down_copy(i):
+        return pltpu.make_async_copy(
+            flip.at[pl.ds(0, width), pl.ds((i % 2) * R, R)],
+            down_out.at[pl.ds(i * width, width)],
+            s.load_sem.at[4 + i % 2],
+        )
+
+    count = F // width
+    for i in range(count):
+        if i >= 2:
+            down_copy(i - 2).wait()
+        flip[:width, (i % 2) * R : (i % 2 + 1) * R] = s.gh[rows, i * width : (i + 1) * width].T
+        down_copy(i).start()
+    for i in range(max(0, count - 2), count):
+        down_copy(i).wait()
+    for step in range(3, n):
+        gather_line_step(2, att_all, step)
+    gather_line_finish(2, s.attt, att_all)
+    share_wait(2, s.gmc)
+
+    def load(i):
+        slot = lax.rem(i, 2)
+        return pltpu.make_async_copy(
+            att_all.at[i // n, lax.rem(i, n)],
+            s.dw.at[pl.ds(pl.multiple_of(slot * QH * H, QH * H), QH * H), pl.ds(0, T)],
+            s.stage_sem.at[slot],
+        )
+
+    load(0).start()
+    outw_out[...] = jnp.zeros(outw_out.shape, F32)
+
+    def step(i, _):
+        @pl.when(i + 1 < 2 * n)
+        def _():
+            load(i + 1).start()
+
+        load(i).wait()
+        slot = lax.rem(i, 2)
+        left = s.dw[pl.ds(pl.multiple_of(slot * QH * H, QH * H), QH * H), pl.ds(0, T)]
+        outw_out[...] += dot(left, s.gmc[:, i].reshape(T, R))
+        return 0
+
+    lax.fori_loop(0, 2 * n, step, 0)
+    chain_final(jobs[1], 1, s.gh.at[rows])
     gate_copy().start()
-    chain_final(out_job, 2, outw_out)
-    gather_line_step(1, qkv_all, n - 1)
+    chain_final(jobs[3], 3, stage)
+    for copy in qkv_copies():
+        copy.start()
     gate_copy().wait()
-    chain_final(up_job, 1, s.gh.at[pl.ds(0, R)])
+    chain_final(jobs[2], 2, s.gh.at[rows])
     up_copy().start()
     for e in range(2):
         for d in range(n):
@@ -748,16 +897,16 @@
         total = total + s.gains_x[i]
     gains_out[...] = total
 
-    gather_line_finish(0, s.hid, hid_all)
-    gather_line_finish(1, s.dqkv, qkv_all)
-    columns_wait_recv(0, s.cott, cott_all)
-    columns_wait_recv(1, s.xt, x1t_all)
-    for b in range(n):
-        job_dp_wait_send(out_job, 2, b)
-    for st in range(n - 1):
-        chain_wait_send(gate_job, 0, st)
-        chain_wait_send(up_job, 1, st)
-        chain_wait_send(out_job, 2, st)
+    columns_wait_send(2, s.gm, s.gmc)
+    mirror(0, s.cot, s.cot2).wait_send()
+    mirror_qkv().wait_send()
+    for d in range(2):
+        mirror_x1(d).wait_send()
+    for b in order:
+        job_dp_wait_send(jobs[-1], len(jobs) - 1, b)
+    for st in range(nl - 1):
+        for k, job in enumerate(jobs):
+            chain_wait_send(job, k, st)
     for r in range(1, reach + 1):
 
         @pl.when((z < n - 1) & (z >= r - 1))
@@ -773,6 +922,8 @@
     spread_wait(5, s.outsh, out_hbm, 0)
     spread_wait(7, s.tgsh, tgrad_hbm, 1)
     up_copy().wait()
+    for copy in qkv_copies():
+        copy.wait()
 
 
 def run_layer(dm, *operands):
@@ -782,27 +933,29 @@
     G = 2 * D + 2 * H
     dma = pltpu.SemaphoreType.DMA
     scratch = dict(
-        tok=((T, D), BF16), x1=((T, D), BF16), cot=((T, D), BF16), x2=((T, D), BF16), gm=((T, D), BF16),
-        outsh=((S, D), BF16), tgsh=((S, D), BF16), xt=((D, T), BF16), cott=((D, T), BF16),
+        tok=((T, D), BF16), x1=((T, D), BF16), send_b=((T, D), BF16), cot=((T, D), BF16), x2=((T, D), BF16),
+        outsh=((S, D), BF16), tgsh=((S, D), BF16), xt=((D // 2, 2 * T), BF16), cott=((D // 2, 2 * T), BF16),
+        cot2=((T, D), BF16), x2b=((T, D), BF16),
         qw=((D, QC), BF16), kw=((D, KV), BF16), vw=((D, KV), BF16), ow=((QC, D), BF16),
         gw=((D, F), BF16), uw=((D, F), BF16), dw=((F, D), BF16),
         tokshare=((S, D), F32), cotshare=((S, D), F32), resid=((S, D), F32), gresid=((S, D), F32),
         k_raw=((T, KV), F32), q_raw=((T, QC), F32), q_rot=((T, QC), BF16), kv=((span, 2 * KV), BF16),
         mask=((T, span), F32), tot=((T, QC), F32), att=((T, QC), F32), att_low=((T, QC), BF16),
-        attt=((QC, T), BF16), gatt=((T, QC), F32), gq_acc=((1, H), F32),
+        attt=((QC, T), BF16), gq_acc=((1, H), F32),
         recv0=((nt - 1, S, D), BF16), recv1=((nt - 1, S, D), BF16),
-        gh=((T, F), F32), hid=((T, F), BF16), gg=((T, F), BF16), gu=((T, F), BF16),
-        dkv=((span, 2 * KV), BF16), dkv_in=((reach, T, 2 * KV), BF16), dqkv=((T, QC + 2 * KV), BF16),
-        chain=((2, 2, n - 1, R, F), BF16),
-        o_recv=((n, QC, R), BF16), o_csend=((n - 1, QC, R), BF16),
-        o_chain=((2, n - 1, QC, R), BF16),
+        gh=((T, F), F32), hid=((2 * T, F), BF16), gg=((2 * T, F), BF16), gu=((2 * T, F), BF16),
+        dkv=((span, 2 * KV), BF16), dkv_in=((reach, T, 2 * KV), BF16), dqkv=((2 * T, QC + 2 * KV), BF16),
+        chain=((4, 1 if n == 4 else 2, n // 2 - 1, R, F), BF16),
+
+        gmc=((nt, 2 * n, S, R), BF16), x1b=((T, D // 2), BF16), x1t=((D // 2, 2 * T), BF16), gh2=((T, F), F32),
+        cos=((T, H), F32), sin=((T, H), F32), segs=((1, reach * T + dm.L), jnp.int32),
         gains=((1, G), F32), gains2=((1, G), F32), gains_p=((nt - 1, 1, G), F32),
         gains_x=((2 * n - 1, 1, G), F32),
     )
     sems = dict(
-        load_sem=(9,), own_sem=(2,), pl_s=(9, nt - 1), pl_r=(9, nt - 1), ag_s=(2, 2, n - 1), ag_r=(2, 2, n - 1),
-        agx_s=(2, 2 * n - 1), agx_r=(2, 2 * n - 1), aa_s=(2, 2 * n), aa_r=(2, 2 * n),
-        dp_s=(3, n), dp_r=(3, n), ch_s=(3, 2, n - 1), ch_r=(3, 2, n - 1), kv_s=(reach,), kv_r=(reach,),
+        load_sem=(9,), own_sem=(3,), pl_s=(13, nt - 1), pl_r=(13, nt - 1), ag_s=(3, 2, n - 1), ag_r=(3, 2, n - 1),
+        agx_s=(3, 2 * n - 1), agx_r=(3, 2 * n - 1), aa_s=(3, 2 * n), aa_r=(3, 2 * n), stage_sem=(2,),
+        dp_s=(4, n // 2), dp_r=(4, n // 2), ch_s=(4, 2, n // 2 - 1, 2), ch_r=(4, 2, n // 2 - 1, 2), mi_s=(5,), mi_r=(5,), kv_s=(reach,), kv_r=(reach,),
         dkv_s=(reach,), dkv_r=(reach,), ga_s=(2 * n,), ga_r=(2 * n,),
     )
     names = list(scratch) + list(sems) + ["credit"]
@@ -827,15 +980,16 @@
             jax.ShapeDtypeStruct((T, D), BF16),
             jax.ShapeDtypeStruct((R, F), F32),
             jax.ShapeDtypeStruct((R, F), F32),
+            jax.ShapeDtypeStruct((F, R), F32),
+            jax.ShapeDtypeStruct((R, QC), F32),
+            jax.ShapeDtypeStruct((R, KV), F32),
+            jax.ShapeDtypeStruct((R, KV), F32),
             jax.ShapeDtypeStruct((QC, R), F32),
-            jax.ShapeDtypeStruct((2, n, T, F), BF16),
-            jax.ShapeDtypeStruct((2, n, T, QC + 2 * KV), BF16),
-            jax.ShapeDtypeStruct((2, n, R, T), BF16),
-            jax.ShapeDtypeStruct((2, n, R, T), BF16),
             jax.ShapeDtypeStruct((1, G), F32),
+            jax.ShapeDtypeStruct((2, n, QC, T), BF16),
         ),
-        in_specs=[hbm] * 2 + [vmem] * 8 + [hbm] * 7,
-        out_specs=[hbm] * 4 + [vmem] + [hbm] * 4 + [vmem],
+        in_specs=[hbm] * 2 + [vmem] * 3 + [hbm] * 7,
+        out_specs=[hbm] * 8 + [vmem] * 2 + [hbm],
         scratch_shapes=shapes,
         compiler_params=pltpu.CompilerParams(
             collective_id=0, has_side_effects=True, vmem_limit_bytes=67043328
@@ -868,33 +1022,19 @@
     length = segments.shape[1]
     dm.reach = -(-(length // 2 - 1) // T)
     dm.S, dm.R = T // dm.nt, D // (2 * dm.n)
-    dm.alias = {"send_b": "x1", "send_a": "tok", "recv2": "recv0", "recv3": "recv1"}
+    dm.alias = {"send_a": "tok", "gm": "x2", "recv2": "recv0", "recv3": "recv1"}
     H = dm.H
-    start = lax.axis_index("ctx") * T
-    row = segments[0]
-    mine = lax.dynamic_slice_in_dim(row, start, T, 0)
-    begins = jnp.sum((row[None, :] < mine[:, None]).astype(jnp.int32), axis=1)
-    position = (start + jnp.arange(T, dtype=jnp.int32) - begins).astype(F32)
-    inverse = 1.0 / rope_base ** (jnp.arange(0, H, 2, dtype=F32) / H)
-    angles = position[:, None] * inverse[None, :]
-    cosine, sine = jnp.cos(angles), jnp.sin(angles)
-    cosine = jnp.concatenate([cosine, cosine], axis=-1)
-    sine = jnp.concatenate([-sine, sine], axis=-1)
-    padded = jnp.concatenate([jnp.full((dm.reach * T,), -1, jnp.int32), row])
-    keys = lax.dynamic_slice_in_dim(padded, start, (dm.reach + 1) * T, 0)
-
-    out, tgrad, gate_g, up_g, out_g, hid, qkv, x1t, cott, gains = run_layer(
+    dm.L = length
+    inverse = (1.0 / rope_base ** (np.arange(0, H, 2, dtype=np.float32) / np.float32(H))).astype(np.float32)
+    inverse = np.concatenate([inverse, inverse])[None]
+    all_gains = jnp.concatenate([first_gain, second_gain, query_norm_gain, key_gain]).astype(F32)[None]
+    out, tgrad, gate_g, up_g, down_g, q_g, k_g, v_g, out_g, gains = run_layer(
         dm,
         tokens.reshape(T, D),
         cotangent.reshape(T, D),
-        first_gain.astype(F32)[None],
-        second_gain.astype(F32)[None],
-        query_norm_gain.astype(F32)[None],
-        key_gain.astype(F32)[None],
-        cosine,
-        sine,
-        mine[:, None],
-        keys[None],
+        all_gains,
+        inverse,
+        segments,
         query_weight,
         key_matrix,
         value_matrix,
@@ -902,19 +1042,15 @@
         gate_weight,
         up_weight,
         down_weight,
-    )
-
-    down_g = jnp.einsum("abtf,abct->fc", hid, cott, preferred_element_type=F32)
-    qkv_g = jnp.einsum("abct,abtm->cm", x1t, qkv, preferred_element_type=F32)
-    QC, KV = dm.QH * H, dm.KH * H
+    )[:10]
     gains = gains[0]
     return (
         out.reshape(tokens.shape),
         tgrad.reshape(tokens.shape),
         gains[:D],
-        qkv_g[:, :QC],
-        qkv_g[:, QC : QC + KV],
-        qkv_g[:, QC + KV :],
+        q_g,
+        k_g,
+        v_g,
         gains[2 * D : 2 * D + H],
         gains[2 * D + H :],
         out_g,

time: 252 us -> 208 us (0.83); the launches traced: 249 us -> 208 us
  Pallas kernels: 223 us -> 191 us
  matrix products: 6.88 us -> 0 us
  other arithmetic: 6.08 us -> 1.3 us
    pallas_call x1, Pallas kernels: 223 us -> 191 us  [run_layer(): pl.pallas_call(body, out_shape=(jax.ShapeDtypeStruct((T, D), BF16), jax.S...]
    dot_general x2 -> x0, matrix products: 6.88 us -> none  [the longest x1 3.9 us: per_device(): qkv_g = jnp.einsum('abct,abtm->cm', x1t, qkv, preferred_element_type=F32)]
    unnamed x19 -> x25, local copies, waits for them, and re-layouts: 5.05 us -> 10.6 us
    broadcast_in_dim x3 -> x0, other arithmetic: 3.76 us -> none  [the longest x1 1.29 us: per_device(): first_gain.astype(F32)[None]]
where the time goes in v1:
time: 208 us
  Pallas kernels  191 us (92%)
  local copies, waits for them, and re-layouts  14.5 us (7%)
    pallas_call x1, Pallas kernels, run_layer(): pl.pallas_call(body, out_shape=(jax.ShapeDtypeStruct((T, D), BF16), jax.S...  191 us
    unnamed x25, local copies, waits for them, and re-layouts  10.6 us

profile of v1, /device:TPU:0, one launch (start us, length us, event | category | flops | bytes accessed | tf_op | source)
XLA Modules:
  0.0 207.8 jit_solution(15608895603884871639)
XLA Ops:
  0.6 0.7 concatenate.18
  1.3 0.7 concatenate.19
  2.0 1.3 maximum_convert_fusion.refs_2_
  3.3 191.2 %layer.1 = (bf16[256,2048]{1,0:T(8,128)(2,1)}, bf16[256,2048]{1,0:T(8,128)(2,1)}, f32[256,1536]{1,0:T(8,128)}, f32[256,1536]{1,0:T(8,128)}, f32[1536,256]{1,0:T(...) custom-call(bf16[256,2048]{1,0:T(8,128)(2,1)} %bitcast.12, ...), custom_call_target="tpu_custom_call" | custom-call | tf_op jit(solution)/shard_map/layer/pallas_call | solution.py:976
  194.6 0.0 copy-start.3
  194.6 1.2 slice_bitcast_fusion
  195.8 1.3 fusion
  197.1 0.0 copy-start.5
  197.1 2.4 %copy.37 = bf16[1,256,2048]{2,1,0:T(8,128)(2,1)} copy(bf16[1,256,2048]{2,1,0:T(8,128)(2,1)} %bitcast.15) | data formatting | bytes 2097152
  199.5 0.0 copy-done.3
  199.5 0.0 copy-start.7
  199.5 0.0 copy-start.6
  199.5 0.0 copy-start.4
  199.5 1.0 copy.38
  200.5 0.0 copy-done.5
  200.5 0.0 copy-start.2
  200.5 0.8 copy.39
  201.3 0.0 copy-done.7
  201.3 0.7 copy.40
  202.0 0.0 copy-done.6
  202.0 0.7 copy.41
  202.7 0.0 copy-done.4
  202.7 0.0 copy-start.1
  202.7 0.8 copy.42
  203.5 0.0 copy-done.2
  203.5 1.1 copy.43
  204.6 0.0 copy-done.1
  204.6 0.0 copy-start
  204.6 1.1 copy.44
  205.8 0.8 copy-done
  206.6 1.1 copy.45
Async XLA Ops:
  194.6 4.9 %copy-start.3 = (bf16[256,2048]{1,0:T(8,128)(2,1)S(1)}, bf16[256,2048]{1,0:T(8,128)(2,1)}, u32[]{:S(2)}) copy-start(bf16[256,2048]{1,0:T(8,128)(2,1)} %get-tuple-element.24) | copy-start | bytes 3145732
  197.1 3.4 %copy-start.5 = (f32[256,512]{1,0:T(8,128)S(1)}, f32[256,512]{1,0:T(8,128)}, u32[]{:S(2)}) copy-start(f32[256,512]{1,0:T(8,128)} %get-tuple-element.53) | copy-start | bytes 1572868
  199.5 1.8 copy-start.7
  199.5 2.5 %copy-start.6 = (f32[256,256]{1,0:T(8,128)S(1)}, f32[256,256]{1,0:T(8,128)}, u32[]{:S(2)}) copy-start(f32[256,256]{1,0:T(8,128)} %get-tuple-element.55) | copy-start | bytes 786436
  199.5 3.2 %copy-start.4 = (f32[512,256]{1,0:T(8,128)S(1)}, f32[512,256]{1,0:T(8,128)}, u32[]{:S(2)}) copy-start(f32[512,256]{1,0:T(8,128)} %get-tuple-element.58) | copy-start | bytes 1572868
  200.5 3.0 %copy-start.2 = (f32[256,1536]{1,0:T(8,128)S(1)}, f32[256,1536]{1,0:T(8,128)}, u32[]{:S(2)}) copy-start(f32[256,1536]{1,0:T(8,128)} %get-tuple-element.60) | copy-start | bytes 4718596
  202.7 1.9 copy-start.1
  204.6 2.0 copy-start

commit v2 on v1

--- a/solution.py
+++ b/solution.py
@@ -58,7 +58,10 @@
     dm,
     tok_hbm,
     cot_hbm,
-    gain_in,
+    first_in,
+    second_in,
+    query_in,
+    key_in,
     inverse,
     seg_row,
     qw_hbm,
@@ -89,6 +92,10 @@
     KV = KH * H
     inv_root = 1.0 / math.sqrt(H)
     C = R // nt
+    gain_in = s.gain_in
+    for place, ref in ((0, first_in), (D, second_in), (2 * D, query_in), (2 * D + H, key_in)):
+        for i in range(ref.shape[0]):
+            gain_in[:, place + i * H : place + (i + 1) * H] = ref[i : i + 1, :].astype(F32)
     g1 = gain_in.at[:, pl.ds(0, D)]
     g2 = gain_in.at[:, pl.ds(D, D)]
     gq = gain_in.at[:, pl.ds(2 * D, H)]
@@ -141,23 +148,45 @@
             total = total + recv[j - 1].astype(F32)
         return total
 
+    def rows_of(peer, half=None):
+        if half is None:
+            return pl.ds(pl.multiple_of(peer * S, S), S)
+        return pl.ds(pl.multiple_of(peer * S + half * (S // 2), S // 2), S // 2)
+
+    def gather_copy(k, full, j):
+        rows = rows_of(t)
+        return remote(full.at[rows], full.at[rows], s.pl_s.at[k, j - 1], s.pl_r.at[k, j - 1], tensor=t ^ j)
+
+    def gather_arrived(k, full, j):
+        rows = rows_of(t ^ j)
+        return remote(full.at[rows], full.at[rows], s.pl_s.at[k, j - 1], s.pl_r.at[k, j - 1], tensor=t ^ j)
+
+    def relay_copy(k, full, origin, half, to):
+        rows = rows_of(origin, half)
+        sems = (s.pl2_s.at[k], s.pl2_r.at[k]) if half else (s.pl_s.at[k, 2], s.pl_r.at[k, 2])
+        return remote(full.at[rows], full.at[rows], *sems, tensor=to)
+
     def gather_start(k, full):
-        mine = pl.ds(pl.multiple_of(t * S, S), S)
-        for j in range(1, nt):
-            remote(
-                full.at[mine], full.at[mine], s.pl_s.at[k, j - 1], s.pl_r.at[k, j - 1], tensor=t ^ j
-            ).start()
+        for j in range(1, nt) if nt != 4 else (1, 2):
+            gather_copy(k, full, j).start()
+
+    def gather_forward(k, full):
+        if nt == 4:
+            gather_arrived(k, full, 1).wait_recv()
+            relay_copy(k, full, t ^ 1, 0, t ^ 2).start()
+            gather_arrived(k, full, 2).wait_recv()
+            relay_copy(k, full, t ^ 2, 1, t ^ 1).start()
 
     def gather_wait(k, full):
-        mine = pl.ds(pl.multiple_of(t * S, S), S)
-        for j in range(1, nt):
-            peer = t ^ j
-            theirs = pl.ds(pl.multiple_of(peer * S, S), S)
-            copy = remote(
-                full.at[mine], full.at[theirs], s.pl_s.at[k, j - 1], s.pl_r.at[k, j - 1], tensor=peer
-            )
-            copy.wait_send()
-            copy.wait_recv()
+        for j in range(1, nt) if nt != 4 else (1, 2):
+            gather_copy(k, full, j).wait_send()
+            if nt != 4:
+                gather_arrived(k, full, j).wait_recv()
+        if nt == 4:
+            relay_copy(k, full, t ^ 1, 0, t ^ 2).wait_send()
+            relay_copy(k, full, t ^ 2, 1, t ^ 1).wait_send()
+            relay_copy(k, full, t ^ 3, 0, t ^ 2).wait_recv()
+            relay_copy(k, full, t ^ 3, 1, t ^ 1).wait_recv()
 
     mine = pl.ds(pl.multiple_of(t * S, S), S)
 
@@ -449,24 +478,25 @@
     own_rows = pl.ds(reach * T, T)
     l_kw.wait()
     l_vw.wait()
-    s.k_raw[...] = dot(s.x1[...], s.kw[...])
-    s.kv[own_rows, KV : 2 * KV] = dot(s.x1[...], s.vw[...]).astype(BF16)
-    for h in range(KH):
-        raw = s.k_raw[:, h * H : (h + 1) * H]
-        s.kv[own_rows, h * H : (h + 1) * H] = rope(raw * rms(raw) * gk[...]).astype(BF16)
-
-    def kv_copy(r):
+    def kv_copy(r, c):
+        lanes = pl.ds(c * 2 * H, 2 * H)
         return remote(
-            s.kv.at[pl.ds((reach - r + 1) * T, T)], s.kv.at[pl.ds((reach - r) * T, T)],
-            s.kv_s.at[r - 1], s.kv_r.at[r - 1], ctx=z + 1,
+            s.kv.at[pl.ds((reach - r + 1) * T, T), lanes], s.kv.at[pl.ds((reach - r) * T, T), lanes],
+            s.kv_s.at[r - 1, c], s.kv_r.at[r - 1, c], ctx=z + 1,
         )
 
-    def kv_send(r):
+    def kv_send(r, c):
         @pl.when((z < n - 1) & (z >= r - 1))
         def _():
-            kv_copy(r).start()
-
-    kv_send(1)
+            kv_copy(r, c).start()
+
+    for h in range(KH):
+        hs = pl.ds(h * H, H)
+        raw = dot(s.x1[...], s.kw[:, hs])
+        s.k_raw[:, hs] = raw
+        s.kv[own_rows, 2 * h * H : (2 * h + 1) * H] = rope(raw * rms(raw) * gk[...]).astype(BF16)
+        s.kv[own_rows, (2 * h + 1) * H : (2 * h + 2) * H] = dot(s.x1[...], s.vw[:, hs]).astype(BF16)
+        kv_send(1, h)
     for r in range(1, reach + 1):
 
         @pl.when(z < r)
@@ -479,13 +509,14 @@
         raw = s.q_raw[:, h * H : (h + 1) * H]
         s.q_rot[:, h * H : (h + 1) * H] = rope(raw * rms(raw) * gq[...]).astype(BF16)
     for r in range(1, reach + 1):
-
-        @pl.when(z >= r)
-        def _():
-            kv_copy(r).wait_recv()
-
-        if r < reach:
-            kv_send(r + 1)
+        for c in range(KH):
+
+            @pl.when(z >= r)
+            def _(r=r, c=c):
+                kv_copy(r, c).wait_recv()
+
+            if r < reach:
+                kv_send(r + 1, c)
     rows_i = lax.broadcasted_iota(jnp.int32, (T, span), 0) + reach * T
     cols_i = lax.broadcasted_iota(jnp.int32, (T, span), 1)
     kseg_f = s.segs[:, pl.ds(pl.multiple_of(z * T, T), span)].astype(F32)
@@ -495,14 +526,14 @@
     def weights_of(h, g):
         hs = pl.ds(pl.multiple_of(h * H, H), H)
         q = s.q_rot[:, hs]
-        k = s.kv[:, pl.ds(pl.multiple_of(g * H, H), H)]
+        k = s.kv[:, pl.ds(pl.multiple_of(2 * g * H, H), H)]
         return q, k, jnp.where(s.mask[...] > 0.0, jnp.exp(dot_nt(q, k) * inv_root), 0.0)
 
     def attend(h, _):
         g = h // group
         hs = pl.ds(pl.multiple_of(h * H, H), H)
         _q, _k, w = weights_of(h, g)
-        v = s.kv[:, pl.ds(pl.multiple_of(KV + g * H, H), H)]
+        v = s.kv[:, pl.ds(pl.multiple_of((2 * g + 1) * H, H), H)]
         total = jnp.sum(w, axis=-1, keepdims=True)
         att = dot(w.astype(BF16), v) / total
         s.tot[:, hs] = jnp.broadcast_to(total, (T, H))
@@ -548,16 +579,17 @@
         gather_start(9, s.cot2)
 
     hidden_grad(s.cot, s.gh)
+    pl.when(z == nl - 1)(lambda: mirror(0, s.cot, s.cot2).start())
 
     s.resid[...] = scatter_sum(0, s.send_a, s.recv0, s.tokshare[...])
     resid = s.resid[...]
     s.x2[mine, :] = (resid * rms(resid) * g2[...]).astype(BF16)
     gather_start(1, s.x2)
     mirror(1, s.x2, s.x2b).start()
-    pl.when(zh == 0)(lambda: mirror(0, s.cot, s.cot2).start())
-    gather_line_start(2, s.attt, att_all)
+    pl.when(z < nl - 1)(lambda: mirror(0, s.cot, s.cot2).start())
     l_gw.wait()
     l_uw.wait()
+    gather_forward(1, s.x2)
     gather_wait(1, s.x2)
 
     def mirrored_share():
@@ -586,6 +618,9 @@
     feed(s.x2, s.gh, 0)
     pl.when(zh == 0)(mirrored_share)
     pl.when(zh == 1)(cot_share)
+    pl.when(zh == 0)(lambda: gather_forward(9, s.cot2))
+    pl.when(zh == 1)(lambda: gather_forward(10, s.x2b))
+    gather_line_start(2, s.attt, att_all)
     for d in range(2):
         mirror_x1(d).start()
     own_part = pl.ds(0, T)
@@ -598,6 +633,8 @@
 
     tiles(D, TILE, body)
     transpose_half(s.x2, s.xt, 0)
+    pl.when(zh == 0)(lambda: gather_forward(10, s.x2b))
+    pl.when(zh == 1)(lambda: gather_forward(9, s.cot2))
     mirror(1, s.x2, s.x2b).wait_send()
     scatter_start(2, s.send_a, s.recv1)
 
@@ -666,8 +703,9 @@
     job_dp_wait_all(jobs[0], 0)
     chain_step(jobs[0], 0, 0, (True, False), (0,))
     chain_step(jobs[0], 0, 0, (True,), (1,))
+    pl.when(zh == 0)(lambda: chain_step(jobs[0], 0, 0, (False,), (1,)))
+    gather_forward(4, s.gm)
     job_dp(1)
-    gather_line_step(2, att_all, 2)
     gather_wait(4, s.gm)
     scatter_start(3, s.send_b, s.recv2)
     for d in range(2):
@@ -689,7 +727,7 @@
     def back(g, _):
         ks = pl.ds(pl.multiple_of(g * H, H), H)
         vs = pl.ds(pl.multiple_of(KV + g * H, H), H)
-        v = s.kv[:, vs]
+        v = s.kv[:, pl.ds(pl.multiple_of((2 * g + 1) * H, H), H)]
         grad_k = jnp.zeros((span, H), F32)
         grad_v = jnp.zeros((span, H), F32)
         for i in range(group):
@@ -739,8 +777,7 @@
             chain_step(jobs[1], 1, 0, (True,))
             job_dp(2)
 
-    chain_step(jobs[0], 0, 0, (False,), (1,))
-    chain_step(jobs[1], 1, 0, (False,))
+    pl.when(zh == 1)(lambda: chain_step(jobs[0], 0, 0, (False,), (1,)))
 
     @pl.when(z < n - 1)
     def _():
@@ -762,6 +799,8 @@
         ).astype(BF16)
     s.gains[:, 2 * D + H :] = gk_sum
     mirror_qkv().start()
+    chain_step(jobs[1], 1, 0, (False,))
+    gather_line_step(2, att_all, 2)
     job_dp_wait_all(jobs[2], 2)
     chain_step(jobs[2], 2, 0)
 
@@ -786,9 +825,17 @@
     scaled = grad_first * g1[...]
     inner = jnp.mean(scaled * normed, axis=-1, keepdims=True)
     s.tgsh[...] = (s.gresid[...] + scale * (scaled - normed * inner)).astype(BF16)
-    spread_start(7, s.tgsh, tgrad_hbm, 1)
     for j in range(1, nt):
         remote(s.gains, s.gains_p.at[j - 1], s.pl_s.at[8, j - 1], s.pl_r.at[8, j - 1], tensor=t ^ j).start()
+    spread_start(7, s.tgsh, tgrad_hbm, 1)
+    mirror_qkv().wait_recv()
+    job_dp(3)
+    job_dp_wait_all(jobs[3], 3)
+    chain_step(jobs[3], 3, 0)
+    for step in range(1, nl - 1):
+        for k, job in enumerate(jobs):
+            chain_step(job, k, step)
+
     columns_wait_recv(2, s.gm, s.gmc)
     share_start(2, s.gmc)
     spread_start(5, s.outsh, out_hbm, 0)
@@ -809,14 +856,6 @@
         for d in range(n):
             if e or d:
                 gain_copy(e, d).start()
-    mirror_qkv().wait_recv()
-    job_dp(3)
-    job_dp_wait_all(jobs[3], 3)
-    chain_step(jobs[3], 3, 0)
-    for step in range(1, nl - 1):
-        for k, job in enumerate(jobs):
-            chain_step(job, k, step)
-
     stage = s.gh2.at[pl.ds(0, R), pl.ds(0, QH * H + 2 * KV)]
 
     def gate_copy():
@@ -910,8 +949,9 @@
     for r in range(1, reach + 1):
 
         @pl.when((z < n - 1) & (z >= r - 1))
-        def _():
-            kv_copy(r).wait_send()
+        def _(r=r):
+            for c in range(KH):
+                kv_copy(r, c).wait_send()
 
     for i in range(reach):
 
@@ -949,13 +989,13 @@
 
         gmc=((nt, 2 * n, S, R), BF16), x1b=((T, D // 2), BF16), x1t=((D // 2, 2 * T), BF16), gh2=((T, F), F32),
         cos=((T, H), F32), sin=((T, H), F32), segs=((1, reach * T + dm.L), jnp.int32),
-        gains=((1, G), F32), gains2=((1, G), F32), gains_p=((nt - 1, 1, G), F32),
+        gain_in=((1, G), F32), gains=((1, G), F32), gains2=((1, G), F32), gains_p=((nt - 1, 1, G), F32),
         gains_x=((2 * n - 1, 1, G), F32),
     )
     sems = dict(
         load_sem=(9,), own_sem=(3,), pl_s=(13, nt - 1), pl_r=(13, nt - 1), ag_s=(3, 2, n - 1), ag_r=(3, 2, n - 1),
         agx_s=(3, 2 * n - 1), agx_r=(3, 2 * n - 1), aa_s=(3, 2 * n), aa_r=(3, 2 * n), stage_sem=(2,),
-        dp_s=(4, n // 2), dp_r=(4, n // 2), ch_s=(4, 2, n // 2 - 1, 2), ch_r=(4, 2, n // 2 - 1, 2), mi_s=(5,), mi_r=(5,), kv_s=(reach,), kv_r=(reach,),
+        dp_s=(4, n // 2), dp_r=(4, n // 2), ch_s=(4, 2, n // 2 - 1, 2), ch_r=(4, 2, n // 2 - 1, 2), mi_s=(5,), mi_r=(5,), kv_s=(reach, KV // H), kv_r=(reach, KV // H), pl2_s=(11,), pl2_r=(11,),
         dkv_s=(reach,), dkv_r=(reach,), ga_s=(2 * n,), ga_r=(2 * n,),
     )
     names = list(scratch) + list(sems) + ["credit"]
@@ -988,7 +1028,7 @@
             jax.ShapeDtypeStruct((1, G), F32),
             jax.ShapeDtypeStruct((2, n, QC, T), BF16),
         ),
-        in_specs=[hbm] * 2 + [vmem] * 3 + [hbm] * 7,
+        in_specs=[hbm] * 2 + [vmem] * 6 + [hbm] * 7,
         out_specs=[hbm] * 8 + [vmem] * 2 + [hbm],
         scratch_shapes=shapes,
         compiler_params=pltpu.CompilerParams(
@@ -996,6 +1036,44 @@
         ),
         name="layer",
     )(*operands)
+
+
+def finish_kernel(dm, *refs):
+    count = len(dm.finish)
+    ins, gains, outs = refs[:count], refs[count], refs[count + 1 : 2 * count + 1]
+    gain_outs = refs[2 * count + 1 : 2 * count + 5]
+    bufs, load_sem, store_sem = refs[2 * count + 5 : 3 * count + 5], refs[-2], refs[-1]
+    loads = [pltpu.make_async_copy(a, b, load_sem.at[i]) for i, (a, b) in enumerate(zip(ins, bufs))]
+    stores = [pltpu.make_async_copy(b, c, store_sem.at[i]) for i, (b, c) in enumerate(zip(bufs, outs))]
+    for load in loads:
+        load.start()
+    place = 0
+    for ref in gain_outs:
+        ref[...] = gains[:, place : place + ref.shape[1]]
+        place += ref.shape[1]
+    for load, store in zip(loads, stores):
+        load.wait()
+        store.start()
+    for store in stores:
+        store.wait()
+
+
+def finish(dm, arrays, gains):
+    dm.finish = arrays
+    hbm = pl.BlockSpec(memory_space=pl.ANY)
+    vmem = pl.BlockSpec(memory_space=pltpu.VMEM)
+    shapes = [jax.ShapeDtypeStruct(a.shape, a.dtype) for a in arrays]
+    gain_shapes = [jax.ShapeDtypeStruct((1, w), F32) for w in (dm.D, dm.D, dm.H, dm.H)]
+    dma = pltpu.SemaphoreType.DMA((len(arrays),))
+    return pl.pallas_call(
+        functools.partial(finish_kernel, dm),
+        out_shape=tuple(shapes + gain_shapes),
+        in_specs=[hbm] * len(arrays) + [vmem],
+        out_specs=tuple([hbm] * len(arrays) + [vmem] * 4),
+        scratch_shapes=[pltpu.VMEM(a.shape, a.dtype) for a in arrays] + [dma, dma],
+        compiler_params=pltpu.CompilerParams(vmem_limit_bytes=67043328),
+        name="finish",
+    )(*arrays, gains)
 
 
 def per_device(
@@ -1027,12 +1105,14 @@
     dm.L = length
     inverse = (1.0 / rope_base ** (np.arange(0, H, 2, dtype=np.float32) / np.float32(H))).astype(np.float32)
     inverse = np.concatenate([inverse, inverse])[None]
-    all_gains = jnp.concatenate([first_gain, second_gain, query_norm_gain, key_gain]).astype(F32)[None]
     out, tgrad, gate_g, up_g, down_g, q_g, k_g, v_g, out_g, gains = run_layer(
         dm,
         tokens.reshape(T, D),
         cotangent.reshape(T, D),
-        all_gains,
+        first_gain.reshape(-1, H),
+        second_gain.reshape(-1, H),
+        query_norm_gain.reshape(1, H),
+        key_gain.reshape(1, H),
         inverse,
         segments,
         query_weight,
@@ -1043,18 +1123,20 @@
         up_weight,
         down_weight,
     )[:10]
-    gains = gains[0]
+    out, tgrad, gate_g, up_g, down_g, q_g, k_g, v_g, out_g, first_g, second_g, qn_g, kn_g = finish(
+        dm, (out, tgrad, gate_g, up_g, down_g, q_g, k_g, v_g, out_g), gains
+    )
     return (
         out.reshape(tokens.shape),
         tgrad.reshape(tokens.shape),
-        gains[:D],
+        first_g.reshape(D),
         q_g,
         k_g,
         v_g,
-        gains[2 * D : 2 * D + H],
-        gains[2 * D + H :],
+        qn_g.reshape(H),
+        kn_g.reshape(H),
         out_g,
-        gains[D : 2 * D],
+        second_g.reshape(D),
         gate_g,
         up_g,
         down_g,

time: 208 us -> 186 us (0.89)
  local copies, waits for them, and re-layouts: 14.5 us -> 0 us
  Pallas kernels: 191 us -> 185 us
    pallas_call x1, Pallas kernels: 191 us -> 177 us  [run_layer(): pl.pallas_call(body, out_shape=(jax.ShapeDtypeStruct((T, D), BF16), jax.S...]
    unnamed x25 -> x0, local copies, waits for them, and re-layouts: 10.6 us -> none
    pallas_call x0 -> x1, Pallas kernels: none -> 7.61 us  [finish(): pl.pallas_call(functools.partial(finish_kernel, dm), out_shape=tuple(shap...]
    slice x2 -> x0, local copies, waits for them, and re-layouts: 2.55 us -> none  [the longest x1 1.32 us: per_device(): gains[D:2 * D]]
where the time goes in v2:
time: 186 us
  Pallas kernels  185 us (99%)
    pallas_call x1, Pallas kernels, run_layer(): pl.pallas_call(body, out_shape=(jax.ShapeDtypeStruct((T, D), BF16), jax.S...  177 us
    pallas_call x1, Pallas kernels, finish(): pl.pallas_call(functools.partial(finish_kernel, dm), out_shape=tuple(shap...  7.61 us

profile of v2, /device:TPU:0, one launch (start us, length us, event | category | flops | bytes accessed | tf_op | source)
XLA Modules:
  0.0 185.7 jit_solution(7795701837126038467)
XLA Ops:
  0.7 177.2 %layer.1 = (bf16[256,2048]{1,0:T(8,128)(2,1)}, bf16[256,2048]{1,0:T(8,128)(2,1)}, f32[256,1536]{1,0:T(8,128)}, f32[256,1536]{1,0:T(8,128)}, f32[1536,256]{1,0:T(...) custom-call(bf16[256,2048]{1,0:T(8,128)(2,1)} %bitcast.12, ...), custom_call_target="tpu_custom_call" | custom-call | tf_op jit(solution)/shard_map/layer/pallas_call | solution.py:1016
  177.9 7.6 %finish.1 = (bf16[256,2048]{1,0:T(8,128)(2,1)}, bf16[256,2048]{1,0:T(8,128)(2,1)}, f32[256,1536]{1,0:T(8,128)}, f32[256,1536]{1,0:T(8,128)}, f32[1536,256]{1,0:T...) custom-call(bf16[256,2048]{1,0:T(8,128)(2,1)} %get-tuple-element.36., ...), custom_call_target="tpu_custom_call" | custom-call | tf_op jit(solution)/shard_map/finish/pallas_call | solution.py:1068

commit v3 on v2

--- a/solution.py
+++ b/solution.py
@@ -129,21 +129,52 @@
         load.start()
     (l_tok, l_cot, l_kw, l_vw, l_qw, l_ow, l_dw, l_gw, l_uw) = loads
 
+    def scatter_direct(k, buf, recv, j):
+        peer = t ^ j
+        return remote(
+            buf.at[pl.ds(pl.multiple_of(peer * S, S), S)], recv.at[j - 1],
+            s.pl_s.at[k, j - 1], s.pl_r.at[k, j - 1], tensor=peer,
+        )
+
+    def scatter_first(k, buf, recv, slot):
+        to = t ^ (1 if slot < 2 else 2)
+        rows = pl.ds(pl.multiple_of((to if slot % 2 == 0 else t ^ 3) * S, S), S)
+        cols = pl.ds(0 if slot < 2 else D // 2, D // 2)
+        return remote(buf.at[rows, cols], recv.at[slot], s.rs_s.at[k, slot], s.rs_r.at[k, slot], tensor=to)
+
+    def scatter_second(k, recv, slot):
+        to = t ^ (2 if slot == 4 else 1)
+        return remote(s.pair.at[slot - 4], recv.at[slot], s.rs_s.at[k, slot], s.rs_r.at[k, slot], tensor=to)
+
     def scatter_start(k, buf, recv):
+        if nt == 4:
+            for slot in (1, 3, 0, 2):
+                scatter_first(k, buf, recv, slot).start()
+        else:
+            for j in range(1, nt):
+                scatter_direct(k, buf, recv, j).start()
+
+    def scatter_sum(k, buf, recv, base):
+        own = pl.ds(pl.multiple_of(t * S, S), S)
+        if nt == 4:
+            for slot, peer, cols in ((1, t ^ 2, slice(0, D // 2)), (3, t ^ 1, slice(D // 2, D))):
+                scatter_first(k, buf, recv, slot).wait_recv()
+                rows = pl.ds(pl.multiple_of(peer * S, S), S)
+                both = buf[rows, cols].astype(F32) + recv[slot].astype(F32)
+                s.pair[slot // 2] = both.astype(BF16)
+                scatter_second(k, recv, 4 + slot // 2).start()
+            for slot in (0, 2):
+                scatter_first(k, buf, recv, slot).wait_recv()
+            for slot in range(4):
+                scatter_first(k, buf, recv, slot).wait_send()
+            for slot in (4, 5):
+                scatter_second(k, recv, slot).wait()
+            left = buf[own, 0 : D // 2].astype(F32) + recv[0].astype(F32) + recv[4].astype(F32)
+            right = buf[own, D // 2 : D].astype(F32) + recv[2].astype(F32) + recv[5].astype(F32)
+            return base + jnp.concatenate([left, right], axis=1)
         for j in range(1, nt):
-            peer = t ^ j
-            remote(
-                buf.at[pl.ds(pl.multiple_of(peer * S, S), S)], recv.at[j - 1],
-                s.pl_s.at[k, j - 1], s.pl_r.at[k, j - 1], tensor=peer,
-            ).start()
-
-    def scatter_sum(k, buf, recv, base):
-        mine = pl.ds(pl.multiple_of(t * S, S), S)
-        for j in range(1, nt):
-            remote(
-                buf.at[mine], recv.at[j - 1], s.pl_s.at[k, j - 1], s.pl_r.at[k, j - 1], tensor=t ^ j
-            ).wait()
-        total = base + buf[mine, :].astype(F32)
+            scatter_direct(k, buf, recv, j).wait()
+        total = base + buf[own, :].astype(F32)
         for j in range(1, nt):
             total = total + recv[j - 1].astype(F32)
         return total
@@ -425,40 +456,23 @@
                     chain_copy(job, k, up, step, part).wait_send()
 
     def chain_final(job, k, out_ref):
-        for up in (True, False):
-            pos = zl if up else zzl
-
-            @pl.when(pos >= 1)
-            def _(up=up):
-                for part in range(2):
+        width = job.cols // 2
+        for part in range(2):
+            for up in (True, False):
+                pos = zl if up else zzl
+
+                @pl.when(pos >= 1)
+                def _(up=up, part=part):
                     chain_copy(job, k, up, nl - 2, part).wait_recv()
 
-        def body(c, w):
-            cs = pl.ds(c, w)
-            total = job.part(dp * nl + zl, c, w) + job.dp_recv(zl)[:, cs].astype(F32)
-            a = job.chain(True, nl - 2)[:, cs].astype(F32)
-            b = job.chain(False, nl - 2)[:, cs].astype(F32)
-            out_ref[:, cs] = total + jnp.where(zl >= 1, a, 0.0) + jnp.where(zzl >= 1, b, 0.0)
-
-        tiles(job.cols, 512, body)
-
-    l_tok.wait()
-    x = s.tok[...].astype(F32)
-    scale = lax.rsqrt(jnp.mean(x * x, axis=-1, keepdims=True) + epsilon)
-    s.x1[...] = (x * scale * g1[...]).astype(BF16)
-    s.tokshare[...] = s.tok[mine, :].astype(F32)
-    l_cot.wait()
-    pl.semaphore_wait(barrier, (nt - 1) + (2 * n - 1))
-    pl.when(zh == 1)(lambda: mirror(0, s.cot, s.cot2).start())
-
-    def rms(v):
-        return lax.rsqrt(jnp.mean(v * v, axis=-1, keepdims=True) + epsilon)
-
-    def rope(v):
-        return v * cos[...] + pltpu.roll(v, H // 2, 1) * sin[...]
-
-    def rope_back(g):
-        return g * cos[...] + pltpu.roll(g * sin[...], H // 2, 1)
+            def body(c, w):
+                cs = pl.ds(pl.multiple_of(part * width + c, 128), w)
+                total = job.part(dp * nl + zl, cs.start, w) + job.dp_recv(zl)[:, cs].astype(F32)
+                a = job.chain(True, nl - 2)[:, cs].astype(F32)
+                b = job.chain(False, nl - 2)[:, cs].astype(F32)
+                out_ref[:, cs] = total + jnp.where(zl >= 1, a, 0.0) + jnp.where(zzl >= 1, b, 0.0)
+
+            tiles(width, 256 if width % 256 == 0 else 128, body)
 
     L = seg_row.shape[1]
     s.segs[:, : reach * T] = jnp.full((1, reach * T), -1, jnp.int32)
@@ -475,6 +489,27 @@
     turned = jnp.sin(angles)
     sin[...] = jnp.where(lane < H // 2, -turned, turned)
 
+    rows_i = lax.broadcasted_iota(jnp.int32, (T, span), 0) + reach * T
+    cols_i = lax.broadcasted_iota(jnp.int32, (T, span), 1)
+    kseg_f = s.segs[:, pl.ds(pl.multiple_of(z * T, T), span)].astype(F32)
+    allowed = (cols_i <= rows_i) & (qseg_f == kseg_f)
+    s.mask[...] = jnp.where(allowed, 1.0, 0.0).astype(F32)
+
+    l_tok.wait()
+    x = s.tok[...].astype(F32)
+    scale = lax.rsqrt(jnp.mean(x * x, axis=-1, keepdims=True) + epsilon)
+    s.x1[...] = (x * scale * g1[...]).astype(BF16)
+    s.tokshare[...] = s.tok[mine, :].astype(F32)
+
+    def rms(v):
+        return lax.rsqrt(jnp.mean(v * v, axis=-1, keepdims=True) + epsilon)
+
+    def rope(v):
+        return v * cos[...] + pltpu.roll(v, H // 2, 1) * sin[...]
+
+    def rope_back(g):
+        return g * cos[...] + pltpu.roll(g * sin[...], H // 2, 1)
+
     own_rows = pl.ds(reach * T, T)
     l_kw.wait()
     l_vw.wait()
@@ -496,7 +531,11 @@
         s.k_raw[:, hs] = raw
         s.kv[own_rows, 2 * h * H : (2 * h + 1) * H] = rope(raw * rms(raw) * gk[...]).astype(BF16)
         s.kv[own_rows, (2 * h + 1) * H : (2 * h + 2) * H] = dot(s.x1[...], s.vw[:, hs]).astype(BF16)
+        if h == 0:
+            pl.semaphore_wait(barrier, (nt - 1) + (2 * n - 1))
         kv_send(1, h)
+    l_cot.wait()
+    pl.when(zh == 1)(lambda: mirror(0, s.cot, s.cot2).start())
     for r in range(1, reach + 1):
 
         @pl.when(z < r)
@@ -517,12 +556,6 @@
 
             if r < reach:
                 kv_send(r + 1, c)
-    rows_i = lax.broadcasted_iota(jnp.int32, (T, span), 0) + reach * T
-    cols_i = lax.broadcasted_iota(jnp.int32, (T, span), 1)
-    kseg_f = s.segs[:, pl.ds(pl.multiple_of(z * T, T), span)].astype(F32)
-    allowed = (cols_i <= rows_i) & (qseg_f == kseg_f)
-    s.mask[...] = jnp.where(allowed, 1.0, 0.0).astype(F32)
-
     def weights_of(h, g):
         hs = pl.ds(pl.multiple_of(h * H, H), H)
         q = s.q_rot[:, hs]
@@ -586,7 +619,6 @@
     s.x2[mine, :] = (resid * rms(resid) * g2[...]).astype(BF16)
     gather_start(1, s.x2)
     mirror(1, s.x2, s.x2b).start()
-    pl.when(z < nl - 1)(lambda: mirror(0, s.cot, s.cot2).start())
     l_gw.wait()
     l_uw.wait()
     gather_forward(1, s.x2)
@@ -616,13 +648,12 @@
         tiles(F, TILE, body)
 
     feed(s.x2, s.gh, 0)
+    pl.when(z < nl - 1)(lambda: mirror(0, s.cot, s.cot2).start())
     pl.when(zh == 0)(mirrored_share)
     pl.when(zh == 1)(cot_share)
     pl.when(zh == 0)(lambda: gather_forward(9, s.cot2))
     pl.when(zh == 1)(lambda: gather_forward(10, s.x2b))
     gather_line_start(2, s.attt, att_all)
-    for d in range(2):
-        mirror_x1(d).start()
     own_part = pl.ds(0, T)
 
     def body(c, w):
@@ -637,6 +668,8 @@
     pl.when(zh == 1)(lambda: gather_forward(9, s.cot2))
     mirror(1, s.x2, s.x2b).wait_send()
     scatter_start(2, s.send_a, s.recv1)
+    for d in range(2):
+        mirror_x1(d).start()
 
     def body(c, w):
         s.send_b[:, pl.ds(c, w)] = dot(s.hid[own_part, :], s.dw[:, pl.ds(c, w)]).astype(BF16)
@@ -701,9 +734,7 @@
     pl.semaphore_wait(s.credit, 1)
     job_dp(0)
     job_dp_wait_all(jobs[0], 0)
-    chain_step(jobs[0], 0, 0, (True, False), (0,))
-    chain_step(jobs[0], 0, 0, (True,), (1,))
-    pl.when(zh == 0)(lambda: chain_step(jobs[0], 0, 0, (False,), (1,)))
+    chain_step(jobs[0], 0, 0)
     gather_forward(4, s.gm)
     job_dp(1)
     gather_wait(4, s.gm)
@@ -775,9 +806,10 @@
         if i == 0:
             job_dp_wait_all(jobs[1], 1)
             chain_step(jobs[1], 1, 0, (True,))
+            pl.when(zh == 0)(lambda: chain_step(jobs[1], 1, 0, (False,), (0,)))
             job_dp(2)
 
-    pl.when(zh == 1)(lambda: chain_step(jobs[0], 0, 0, (False,), (1,)))
+    pl.when(zh == 0)(lambda: chain_step(jobs[1], 1, 0, (False,), (1,)))
 
     @pl.when(z < n - 1)
     def _():
@@ -798,12 +830,13 @@
             r * (sc - nk * jnp.mean(sc * nk, axis=-1, keepdims=True))
         ).astype(BF16)
     s.gains[:, 2 * D + H :] = gk_sum
+    pl.when(zh == 1)(lambda: chain_step(jobs[1], 1, 0, (False,)))
     mirror_qkv().start()
-    chain_step(jobs[1], 1, 0, (False,))
     gather_line_step(2, att_all, 2)
     job_dp_wait_all(jobs[2], 2)
     chain_step(jobs[2], 2, 0)
 
+    s.outsh[...] = scatter_sum(3, s.send_b, s.recv2, s.resid[...]).astype(BF16)
     q_c, k_c, v_c = pl.ds(0, QH * H), pl.ds(QH * H, KV), pl.ds(QH * H + KV, KV)
 
     def body(c, w):
@@ -816,7 +849,6 @@
 
     tiles(D, TILE, body)
     scatter_start(6, s.send_a, s.recv3)
-    s.outsh[...] = scatter_sum(3, s.send_b, s.recv2, s.resid[...]).astype(BF16)
     grad_first = scatter_sum(6, s.send_a, s.recv3, jnp.zeros((S, D), F32))
     tokshare = s.tokshare[...]
     scale = rms(tokshare)
@@ -828,17 +860,6 @@
     for j in range(1, nt):
         remote(s.gains, s.gains_p.at[j - 1], s.pl_s.at[8, j - 1], s.pl_r.at[8, j - 1], tensor=t ^ j).start()
     spread_start(7, s.tgsh, tgrad_hbm, 1)
-    mirror_qkv().wait_recv()
-    job_dp(3)
-    job_dp_wait_all(jobs[3], 3)
-    chain_step(jobs[3], 3, 0)
-    for step in range(1, nl - 1):
-        for k, job in enumerate(jobs):
-            chain_step(job, k, step)
-
-    columns_wait_recv(2, s.gm, s.gmc)
-    share_start(2, s.gmc)
-    spread_start(5, s.outsh, out_hbm, 0)
     for j in range(1, nt):
         remote(s.gains, s.gains_p.at[j - 1], s.pl_s.at[8, j - 1], s.pl_r.at[8, j - 1], tensor=t ^ j).wait()
     total = s.gains[...]
@@ -856,6 +877,9 @@
         for d in range(n):
             if e or d:
                 gain_copy(e, d).start()
+    columns_wait_recv(2, s.gm, s.gmc)
+    share_start(2, s.gmc)
+    spread_start(5, s.outsh, out_hbm, 0)
     stage = s.gh2.at[pl.ds(0, R), pl.ds(0, QH * H + 2 * KV)]
 
     def gate_copy():
@@ -871,6 +895,9 @@
             for i, (ref, a, w) in enumerate(parts)
         ]
 
+    for step in range(1, nl - 1):
+        for k in range(3):
+            chain_step(jobs[k], k, step)
     rows = pl.ds(0, R)
     chain_final(jobs[0], 0, s.gh.at[rows])
     width = min(256, F)
@@ -891,6 +918,16 @@
         down_copy(i).start()
     for i in range(max(0, count - 2), count):
         down_copy(i).wait()
+    mirror_qkv().wait_recv()
+    job_dp(3)
+    job_dp_wait_all(jobs[3], 3)
+    chain_step(jobs[3], 3, 0)
+    for step in range(1, nl - 1):
+        chain_step(jobs[3], 3, step)
+
+
+    chain_final(jobs[1], 1, s.gh.at[rows])
+    gate_copy().start()
     for step in range(3, n):
         gather_line_step(2, att_all, step)
     gather_line_finish(2, s.attt, att_all)
@@ -905,7 +942,7 @@
         )
 
     load(0).start()
-    outw_out[...] = jnp.zeros(outw_out.shape, F32)
+    s.outw[...] = jnp.zeros(s.outw.shape, F32)
 
     def step(i, _):
         @pl.when(i + 1 < 2 * n)
@@ -915,18 +952,21 @@
         load(i).wait()
         slot = lax.rem(i, 2)
         left = s.dw[pl.ds(pl.multiple_of(slot * QH * H, QH * H), QH * H), pl.ds(0, T)]
-        outw_out[...] += dot(left, s.gmc[:, i].reshape(T, R))
+        s.outw[...] += dot(left, s.gmc[:, i].reshape(T, R))
         return 0
 
     lax.fori_loop(0, 2 * n, step, 0)
-    chain_final(jobs[1], 1, s.gh.at[rows])
-    gate_copy().start()
+
+    def outw_copy():
+        return pltpu.make_async_copy(s.outw, outw_out, s.load_sem.at[4])
+
+    outw_copy().start()
+    gate_copy().wait()
+    chain_final(jobs[2], 2, s.gh.at[rows])
+    up_copy().start()
     chain_final(jobs[3], 3, stage)
     for copy in qkv_copies():
         copy.start()
-    gate_copy().wait()
-    chain_final(jobs[2], 2, s.gh.at[rows])
-    up_copy().start()
     for e in range(2):
         for d in range(n):
             if e or d:
@@ -962,6 +1002,7 @@
     spread_wait(5, s.outsh, out_hbm, 0)
     spread_wait(7, s.tgsh, tgrad_hbm, 1)
     up_copy().wait()
+    outw_copy().wait()
     for copy in qkv_copies():
         copy.wait()
 
@@ -982,20 +1023,21 @@
         k_raw=((T, KV), F32), q_raw=((T, QC), F32), q_rot=((T, QC), BF16), kv=((span, 2 * KV), BF16),
         mask=((T, span), F32), tot=((T, QC), F32), att=((T, QC), F32), att_low=((T, QC), BF16),
         attt=((QC, T), BF16), gq_acc=((1, H), F32),
-        recv0=((nt - 1, S, D), BF16), recv1=((nt - 1, S, D), BF16),
+        recv0=((6, S, D // 2) if nt == 4 else (nt - 1, S, D), BF16),
+        recv1=((6, S, D // 2) if nt == 4 else (nt - 1, S, D), BF16), pair=((2, S, D // 2), BF16),
         gh=((T, F), F32), hid=((2 * T, F), BF16), gg=((2 * T, F), BF16), gu=((2 * T, F), BF16),
         dkv=((span, 2 * KV), BF16), dkv_in=((reach, T, 2 * KV), BF16), dqkv=((2 * T, QC + 2 * KV), BF16),
         chain=((4, 1 if n == 4 else 2, n // 2 - 1, R, F), BF16),
 
         gmc=((nt, 2 * n, S, R), BF16), x1b=((T, D // 2), BF16), x1t=((D // 2, 2 * T), BF16), gh2=((T, F), F32),
         cos=((T, H), F32), sin=((T, H), F32), segs=((1, reach * T + dm.L), jnp.int32),
-        gain_in=((1, G), F32), gains=((1, G), F32), gains2=((1, G), F32), gains_p=((nt - 1, 1, G), F32),
+        outw=((QC, R), F32), gain_in=((1, G), F32), gains=((1, G), F32), gains2=((1, G), F32), gains_p=((nt - 1, 1, G), F32),
         gains_x=((2 * n - 1, 1, G), F32),
     )
     sems = dict(
         load_sem=(9,), own_sem=(3,), pl_s=(13, nt - 1), pl_r=(13, nt - 1), ag_s=(3, 2, n - 1), ag_r=(3, 2, n - 1),
         agx_s=(3, 2 * n - 1), agx_r=(3, 2 * n - 1), aa_s=(3, 2 * n), aa_r=(3, 2 * n), stage_sem=(2,),
-        dp_s=(4, n // 2), dp_r=(4, n // 2), ch_s=(4, 2, n // 2 - 1, 2), ch_r=(4, 2, n // 2 - 1, 2), mi_s=(5,), mi_r=(5,), kv_s=(reach, KV // H), kv_r=(reach, KV // H), pl2_s=(11,), pl2_r=(11,),
+        dp_s=(4, n // 2), dp_r=(4, n // 2), ch_s=(4, 2, n // 2 - 1, 2), ch_r=(4, 2, n // 2 - 1, 2), mi_s=(5,), mi_r=(5,), kv_s=(reach, KV // H), kv_r=(reach, KV // H), pl2_s=(11,), pl2_r=(11,), rs_s=(7, 6), rs_r=(7, 6),
         dkv_s=(reach,), dkv_r=(reach,), ga_s=(2 * n,), ga_r=(2 * n,),
     )
     names = list(scratch) + list(sems) + ["credit"]
@@ -1029,7 +1071,7 @@
             jax.ShapeDtypeStruct((2, n, QC, T), BF16),
         ),
         in_specs=[hbm] * 2 + [vmem] * 6 + [hbm] * 7,
-        out_specs=[hbm] * 8 + [vmem] * 2 + [hbm],
+        out_specs=[hbm] * 9 + [vmem] + [hbm],
         scratch_shapes=shapes,
         compiler_params=pltpu.CompilerParams(
             collective_id=0, has_side_effects=True, vmem_limit_bytes=67043328
@@ -1038,22 +1080,37 @@
     )(*operands)
 
 
+FINISH_WINDOW = 64
+
+
+def finish_pieces(shape):
+    rows = shape[0]
+    step = rows // 2 if rows % 32 == 0 else rows
+    return [(r, step) for r in range(0, rows, step)]
+
+
 def finish_kernel(dm, *refs):
     count = len(dm.finish)
     ins, gains, outs = refs[:count], refs[count], refs[count + 1 : 2 * count + 1]
     gain_outs = refs[2 * count + 1 : 2 * count + 5]
     bufs, load_sem, store_sem = refs[2 * count + 5 : 3 * count + 5], refs[-2], refs[-1]
-    loads = [pltpu.make_async_copy(a, b, load_sem.at[i]) for i, (a, b) in enumerate(zip(ins, bufs))]
-    stores = [pltpu.make_async_copy(b, c, store_sem.at[i]) for i, (b, c) in enumerate(zip(bufs, outs))]
-    for load in loads:
+    loads, stores = [], []
+    for a, b, c in zip(ins, bufs, outs):
+        for start, size in finish_pieces(a.shape):
+            rows, i = pl.ds(start, size), len(loads)
+            loads.append(pltpu.make_async_copy(a.at[rows], b.at[rows], load_sem.at[i]))
+            stores.append(pltpu.make_async_copy(b.at[rows], c.at[rows], store_sem.at[i]))
+    for load in loads[:FINISH_WINDOW]:
         load.start()
     place = 0
     for ref in gain_outs:
         ref[...] = gains[:, place : place + ref.shape[1]]
         place += ref.shape[1]
-    for load, store in zip(loads, stores):
+    for i, (load, store) in enumerate(zip(loads, stores)):
         load.wait()
         store.start()
+        if i + FINISH_WINDOW < len(loads):
+            loads[i + FINISH_WINDOW].start()
     for store in stores:
         store.wait()
 
@@ -1064,7 +1121,7 @@
     vmem = pl.BlockSpec(memory_space=pltpu.VMEM)
     shapes = [jax.ShapeDtypeStruct(a.shape, a.dtype) for a in arrays]
     gain_shapes = [jax.ShapeDtypeStruct((1, w), F32) for w in (dm.D, dm.D, dm.H, dm.H)]
-    dma = pltpu.SemaphoreType.DMA((len(arrays),))
+    dma = pltpu.SemaphoreType.DMA((sum(len(finish_pieces(a.shape)) for a in arrays),))
     return pl.pallas_call(
         functools.partial(finish_kernel, dm),
         out_shape=tuple(shapes + gain_shapes),

time: 186 us -> 183 us (0.984)
  Pallas kernels: 185 us -> 181 us
    pallas_call x1, Pallas kernels: 177 us -> 174 us  [run_layer(): pl.pallas_call(body, out_shape=(jax.ShapeDtypeStruct((T, D), BF16), jax.S...]
where the time goes in v3:
time: 183 us; the launch traced here: 182 us
  Pallas kernels  181 us (99%)
    pallas_call x1, Pallas kernels, run_layer(): pl.pallas_call(body, out_shape=(jax.ShapeDtypeStruct((T, D), BF16), jax.S...  174 us
    pallas_call x1, Pallas kernels, finish(): pl.pallas_call(functools.partial(finish_kernel, dm), out_shape=tuple(shap...  7.59 us

profile of v3, /device:TPU:0, one launch (start us, length us, event | category | flops | bytes accessed | tf_op | source)
XLA Modules:
  0.0 182.1 jit_solution(16648098300830045215)
XLA Ops:
  0.7 173.7 %layer.1 = (bf16[256,2048]{1,0:T(8,128)(2,1)}, bf16[256,2048]{1,0:T(8,128)(2,1)}, f32[256,1536]{1,0:T(8,128)}, f32[256,1536]{1,0:T(8,128)}, f32[1536,256]{1,0:T(...) custom-call(bf16[256,2048]{1,0:T(8,128)(2,1)} %bitcast.12, ...), custom_call_target="tpu_custom_call" | custom-call | tf_op jit(solution)/shard_map/layer/pallas_call | solution.py:1058
  174.4 7.6 %finish.1 = (bf16[256,2048]{1,0:T(8,128)(2,1)}, bf16[256,2048]{1,0:T(8,128)(2,1)}, f32[256,1536]{1,0:T(8,128)}, f32[256,1536]{1,0:T(8,128)}, f32[1536,256]{1,0:T...) custom-call(bf16[256,2048]{1,0:T(8,128)(2,1)} %get-tuple-element.36., ...), custom_call_target="tpu_custom_call" | custom-call | tf_op jit(solution)/shard_map/finish/pallas_call | solution.py:1125

commit v4 on v3

--- a/solution.py
+++ b/solution.py
@@ -622,14 +622,14 @@
     l_gw.wait()
     l_uw.wait()
     gather_forward(1, s.x2)
+    pl.when(z < nl - 1)(lambda: mirror(0, s.cot, s.cot2).start())
     gather_wait(1, s.x2)
 
     def mirrored_share():
         mirror(1, s.x2, s.x2b).wait_recv()
         gather_start(10, s.x2b)
 
-    pl.when(zh == 1)(mirrored_share)
-    pl.when(zh == 0)(cot_share)
+    cot_share()
 
     def feed(x, grad_hidden, place):
         rows = pl.ds(place * T, T)
@@ -648,11 +648,8 @@
         tiles(F, TILE, body)
 
     feed(s.x2, s.gh, 0)
-    pl.when(z < nl - 1)(lambda: mirror(0, s.cot, s.cot2).start())
-    pl.when(zh == 0)(mirrored_share)
-    pl.when(zh == 1)(cot_share)
-    pl.when(zh == 0)(lambda: gather_forward(9, s.cot2))
-    pl.when(zh == 1)(lambda: gather_forward(10, s.x2b))
+    mirrored_share()
+    gather_forward(9, s.cot2)
     gather_line_start(2, s.attt, att_all)
     own_part = pl.ds(0, T)
 
@@ -664,8 +661,7 @@
 
     tiles(D, TILE, body)
     transpose_half(s.x2, s.xt, 0)
-    pl.when(zh == 0)(lambda: gather_forward(10, s.x2b))
-    pl.when(zh == 1)(lambda: gather_forward(9, s.cot2))
+    gather_forward(10, s.x2b)
     mirror(1, s.x2, s.x2b).wait_send()
     scatter_start(2, s.send_a, s.recv1)
     for d in range(2):
@@ -681,7 +677,6 @@
     gather_wait(10, s.x2b)
     feed(s.x2b, s.gh2, 1)
     transpose_half(s.x2b, s.xt, 1)
-    gather_line_step(2, att_all, 1)
     pl.semaphore_signal(s.credit, inc=1, device_id={"dp": 1 - dp}, device_id_type=MESH)
 
     grad_second = scatter_sum(2, s.send_a, s.recv1, jnp.zeros((S, D), F32))
@@ -736,6 +731,7 @@
     job_dp_wait_all(jobs[0], 0)
     chain_step(jobs[0], 0, 0)
     gather_forward(4, s.gm)
+    gather_line_step(2, att_all, 1)
     job_dp(1)
     gather_wait(4, s.gm)
     scatter_start(3, s.send_b, s.recv2)
@@ -974,7 +970,12 @@
     total = s.gains2[...]
     for i in range(2 * n - 1):
         total = total + s.gains_x[i]
-    gains_out[...] = total
+    s.gains[...] = total
+
+    def gains_copy():
+        return pltpu.make_async_copy(s.gains, gains_out, s.load_sem.at[2])
+
+    gains_copy().start()
 
     columns_wait_send(2, s.gm, s.gmc)
     mirror(0, s.cot, s.cot2).wait_send()
@@ -1001,6 +1002,7 @@
 
     spread_wait(5, s.outsh, out_hbm, 0)
     spread_wait(7, s.tgsh, tgrad_hbm, 1)
+    gains_copy().wait()
     up_copy().wait()
     outw_copy().wait()
     for copy in qkv_copies():
@@ -1071,7 +1073,7 @@
             jax.ShapeDtypeStruct((2, n, QC, T), BF16),
         ),
         in_specs=[hbm] * 2 + [vmem] * 6 + [hbm] * 7,
-        out_specs=[hbm] * 9 + [vmem] + [hbm],
+        out_specs=[hbm] * 11,
         scratch_shapes=shapes,
         compiler_params=pltpu.CompilerParams(
             collective_id=0, has_side_effects=True, vmem_limit_bytes=67043328

time: 183 us -> 183 us (level)
  no operation moved by 1% of the time
where the time goes in v4:
time: 183 us; the launch traced here: 181 us
  Pallas kernels  180 us (98%)
    pallas_call x1, Pallas kernels, run_layer(): pl.pallas_call(body, out_shape=(jax.ShapeDtypeStruct((T, D), BF16), jax.S...  173 us
    pallas_call x1, Pallas kernels, finish(): pl.pallas_call(functools.partial(finish_kernel, dm), out_shape=tuple(shap...  7.59 us

profile of v4, /device:TPU:0, one launch (start us, length us, event | category | flops | bytes accessed | tf_op | source)
XLA Modules:
  0.0 181.1 jit_solution(3034609490431882949)
XLA Ops:
  0.7 172.7 %layer.1 = (bf16[256,2048]{1,0:T(8,128)(2,1)}, bf16[256,2048]{1,0:T(8,128)(2,1)}, f32[256,1536]{1,0:T(8,128)}, f32[256,1536]{1,0:T(8,128)}, f32[1536,256]{1,0:T(...) custom-call(bf16[256,2048]{1,0:T(8,128)(2,1)} %bitcast.12, ...), custom_call_target="tpu_custom_call" | custom-call | tf_op jit(solution)/shard_map/layer/pallas_call | solution.py:1060
  173.4 7.6 %finish.1 = (bf16[256,2048]{1,0:T(8,128)(2,1)}, bf16[256,2048]{1,0:T(8,128)(2,1)}, f32[256,1536]{1,0:T(8,128)}, f32[256,1536]{1,0:T(8,128)}, f32[1536,256]{1,0:T...) custom-call(bf16[256,2048]{1,0:T(8,128)(2,1)} %get-tuple-element.36., ...), custom_call_target="tpu_custom_call" | custom-call | tf_op jit(solution)/shard_map/finish/pallas_call | solution.py:1127

commit v5 on v4

--- a/solution.py
+++ b/solution.py
@@ -269,43 +269,37 @@
             ref if src is None else src, ref, s.agx_s.at[k, slot], s.agx_r.at[k, slot], dp=1 - dp
         )
 
-    def gather_line_start(k, src, all_ref):
-        pltpu.make_async_copy(src, all_ref.at[dp, z], s.own_sem.at[k]).start()
-
-        @pl.when(z < n - 1)
-        def _():
-            line_copy(k, all_ref, True, 0, src).start()
-
-        @pl.when(z > 0)
-        def _():
-            line_copy(k, all_ref, False, 0, src).start()
-
-        core_copy(k, all_ref, 0, z, src).start()
-
-    def gather_line_step(k, all_ref, step):
-        @pl.when(z >= step)
-        def _():
-            ref = all_ref.at[dp, z - step]
-            remote(ref, ref, s.ag_s.at[k, 0, step - 1], s.ag_r.at[k, 0, step - 1], ctx=z - 1).wait_recv()
-            if step < n - 1:
-
-                @pl.when(z < n - 1)
-                def _():
-                    line_copy(k, all_ref, True, step).start()
-
-            core_copy(k, all_ref, step, z - step).start()
-
-        @pl.when(zz >= step)
-        def _():
-            ref = all_ref.at[dp, z + step]
-            remote(ref, ref, s.ag_s.at[k, 1, step - 1], s.ag_r.at[k, 1, step - 1], ctx=z + 1).wait_recv()
-            if step < n - 1:
-
-                @pl.when(z > 0)
-                def _():
-                    line_copy(k, all_ref, False, step).start()
-
-            core_copy(k, all_ref, n - 1 + step, z + step).start()
+    def gather_line_start(k, src, all_ref, ways, own):
+        if own:
+            pltpu.make_async_copy(src, all_ref.at[dp, z], s.own_sem.at[k]).start()
+        for up in ways:
+
+            @pl.when((z < n - 1) if up else (z > 0))
+            def _(up=up):
+                line_copy(k, all_ref, up, 0, src).start()
+
+        if own:
+            core_copy(k, all_ref, 0, z, src).start()
+
+    def gather_line_step(k, all_ref, step, ways=(True, False)):
+        for up in ways:
+
+            @pl.when((z >= step) if up else (zz >= step))
+            def _(up=up):
+                idx = (z - step) if up else (z + step)
+                ref = all_ref.at[dp, idx]
+                i = 0 if up else 1
+                remote(
+                    ref, ref, s.ag_s.at[k, i, step - 1], s.ag_r.at[k, i, step - 1],
+                    ctx=(z - 1) if up else (z + 1),
+                ).wait_recv()
+                if step < n - 1:
+
+                    @pl.when((z < n - 1) if up else (z > 0))
+                    def _():
+                        line_copy(k, all_ref, up, step).start()
+
+                core_copy(k, all_ref, step if up else n - 1 + step, idx).start()
 
     def gather_line_finish(k, src, all_ref):
         pltpu.make_async_copy(src, all_ref.at[dp, z], s.own_sem.at[k]).wait()
@@ -584,6 +578,7 @@
 
     tiles(D, TILE, body)
     scatter_start(0, s.send_a, s.recv0)
+    gather_line_start(2, s.attt, att_all, (False,), True)
 
     def transpose_half(src, dst, place):
         for d in range(2):
@@ -619,6 +614,7 @@
     s.x2[mine, :] = (resid * rms(resid) * g2[...]).astype(BF16)
     gather_start(1, s.x2)
     mirror(1, s.x2, s.x2b).start()
+    gather_line_step(2, att_all, 1, (False,))
     l_gw.wait()
     l_uw.wait()
     gather_forward(1, s.x2)
@@ -650,7 +646,8 @@
     feed(s.x2, s.gh, 0)
     mirrored_share()
     gather_forward(9, s.cot2)
-    gather_line_start(2, s.attt, att_all)
+    gather_line_start(2, s.attt, att_all, (True,), False)
+    gather_line_step(2, att_all, 2, (False,))
     own_part = pl.ds(0, T)
 
     def body(c, w):
@@ -731,7 +728,7 @@
     job_dp_wait_all(jobs[0], 0)
     chain_step(jobs[0], 0, 0)
     gather_forward(4, s.gm)
-    gather_line_step(2, att_all, 1)
+    gather_line_step(2, att_all, 1, (True,))
     job_dp(1)
     gather_wait(4, s.gm)
     scatter_start(3, s.send_b, s.recv2)
@@ -828,7 +825,7 @@
     s.gains[:, 2 * D + H :] = gk_sum
     pl.when(zh == 1)(lambda: chain_step(jobs[1], 1, 0, (False,)))
     mirror_qkv().start()
-    gather_line_step(2, att_all, 2)
+    gather_line_step(2, att_all, 2, (True,))
     job_dp_wait_all(jobs[2], 2)
     chain_step(jobs[2], 2, 0)
 

time: 183 us -> 181 us (0.989)
  no operation moved by 1% of the time
where the time goes in v5:
time: 181 us; the launch traced here: 180 us
  Pallas kernels  180 us (99%)
    pallas_call x1, Pallas kernels, run_layer(): pl.pallas_call(body, out_shape=(jax.ShapeDtypeStruct((T, D), BF16), jax.S...  172 us
    pallas_call x1, Pallas kernels, finish(): pl.pallas_call(functools.partial(finish_kernel, dm), out_shape=tuple(shap...  7.59 us

profile of v5, /device:TPU:0, one launch (start us, length us, event | category | flops | bytes accessed | tf_op | source)
XLA Modules:
  0.0 180.3 jit_solution(12723757267515897201)
XLA Ops:
  0.7 171.9 %layer.1 = (bf16[256,2048]{1,0:T(8,128)(2,1)}, bf16[256,2048]{1,0:T(8,128)(2,1)}, f32[256,1536]{1,0:T(8,128)}, f32[256,1536]{1,0:T(8,128)}, f32[1536,256]{1,0:T(...) custom-call(bf16[256,2048]{1,0:T(8,128)(2,1)} %bitcast.12, ...), custom_call_target="tpu_custom_call" | custom-call | tf_op jit(solution)/shard_map/layer/pallas_call | solution.py:1057
  172.6 7.6 %finish.1 = (bf16[256,2048]{1,0:T(8,128)(2,1)}, bf16[256,2048]{1,0:T(8,128)(2,1)}, f32[256,1536]{1,0:T(8,128)}, f32[256,1536]{1,0:T(8,128)}, f32[1536,256]{1,0:T...) custom-call(bf16[256,2048]{1,0:T(8,128)(2,1)} %get-tuple-element.36., ...), custom_call_target="tpu_custom_call" | custom-call | tf_op jit(solution)/shard_map/finish/pallas_call | solution.py:1124

commit v6 on v5

--- a/solution.py
+++ b/solution.py
@@ -830,6 +830,7 @@
     chain_step(jobs[2], 2, 0)
 
     s.outsh[...] = scatter_sum(3, s.send_b, s.recv2, s.resid[...]).astype(BF16)
+    spread_start(5, s.outsh, out_hbm, 0)
     q_c, k_c, v_c = pl.ds(0, QH * H), pl.ds(QH * H, KV), pl.ds(QH * H + KV, KV)
 
     def body(c, w):
@@ -872,7 +873,6 @@
                 gain_copy(e, d).start()
     columns_wait_recv(2, s.gm, s.gmc)
     share_start(2, s.gmc)
-    spread_start(5, s.outsh, out_hbm, 0)
     stage = s.gh2.at[pl.ds(0, R), pl.ds(0, QH * H + 2 * KV)]
 
     def gate_copy():

time: 181 us -> 186 us (1.028)
  Pallas kernels: 180 us -> 185 us
    pallas_call x1, Pallas kernels: 172 us -> 178 us  [run_layer(): pl.pallas_call(body, out_shape=(jax.ShapeDtypeStruct((T, D), BF16), jax.S...]
where the time goes in v6:
time: 186 us
  Pallas kernels  185 us (99%)
    pallas_call x1, Pallas kernels, run_layer(): pl.pallas_call(body, out_shape=(jax.ShapeDtypeStruct((T, D), BF16), jax.S...  178 us
    pallas_call x1, Pallas kernels, finish(): pl.pallas_call(functools.partial(finish_kernel, dm), out_shape=tuple(shap...  7.59 us

profile of v6, /device:TPU:0, one launch (start us, length us, event | category | flops | bytes accessed | tf_op | source)
XLA Modules:
  0.0 185.9 jit_solution(8192272601283958088)
XLA Ops:
  0.7 177.5 %layer.1 = (bf16[256,2048]{1,0:T(8,128)(2,1)}, bf16[256,2048]{1,0:T(8,128)(2,1)}, f32[256,1536]{1,0:T(8,128)}, f32[256,1536]{1,0:T(8,128)}, f32[1536,256]{1,0:T(...) custom-call(bf16[256,2048]{1,0:T(8,128)(2,1)} %bitcast.12, ...), custom_call_target="tpu_custom_call" | custom-call | tf_op jit(solution)/shard_map/layer/pallas_call | solution.py:1057
  178.2 7.6 %finish.1 = (bf16[256,2048]{1,0:T(8,128)(2,1)}, bf16[256,2048]{1,0:T(8,128)(2,1)}, f32[256,1536]{1,0:T(8,128)}, f32[256,1536]{1,0:T(8,128)}, f32[1536,256]{1,0:T...) custom-call(bf16[256,2048]{1,0:T(8,128)(2,1)} %get-tuple-element.36., ...), custom_call_target="tpu_custom_call" | custom-call | tf_op jit(solution)/shard_map/finish/pallas_call | solution.py:1124
